TPU v7x, 32 devices: a 4x4x1 block of a 4x4x8 slice. The times are simulated.
32 devices in a mesh: dp: 1 (over z), sp: 32 (over y, x, core).
Axes of the slice: x: 4, y: 4, z: 1, core: 2. Of those that a mesh axis runs over, the one named last changes fastest.
The devices are a block of a 4x4x8 slice.
Arguments:
- images: bfloat16 [32, 64, 512, 32], P('dp', 'sp')
- w_a: bfloat16 [1, 3, 3, 32, 32], replicated
- bn_a: float32 [1, 2, 32], replicated
- w_down: bfloat16 [3, 3, 32, 128], replicated
- bn_down: float32 [2, 128], replicated
- w_in: bfloat16 [3, 128, 64], replicated
- bn_in: float32 [3, 2, 64], replicated
- w_mid: bfloat16 [3, 3, 3, 64, 64], replicated
- bn_mid: float32 [3, 2, 64], replicated
- w_out: bfloat16 [3, 64, 128], replicated
- bn_out: float32 [3, 2, 128], replicated
Outputs:
- output: bfloat16 [32, 32, 256, 128], P('dp', 'sp')
All inputs are finite; a program needn't handle non-finite values.
Results may differ from a plain program's by a relative error of at most 0.0190335.
Values are sent between devices in bfloat16 or wider.
A program may use at most 768 MiB of HBM per device.

v0:
```python
import jax
import jax.numpy as jnp
from jax import lax
from jax.sharding import PartitionSpec as P, NamedSharding

NORM_EPS = 1e-5
CONV_DIMS = ("NHWC", "HWIO", "NHWC")


def solution(mesh):
    groups = mesh.shape["sp"]
    to_next = [(device, device + 1) for device in range(groups - 1)]
    to_prev = [(device + 1, device) for device in range(groups - 1)]

    def conv_same(hidden, weight):
        from_above = lax.ppermute(hidden[:, -1:], "sp", to_next)
        from_below = lax.ppermute(hidden[:, :1], "sp", to_prev)
        padded = jnp.concatenate([from_above, hidden, from_below], axis=1)
        return lax.conv_general_dilated(padded, weight, (1, 1), ((0, 0), (1, 1)), dimension_numbers=CONV_DIMS, preferred_element_type=jnp.float32)

    def conv_down(hidden, weight):
        from_below = lax.ppermute(hidden[:, :1], "sp", to_prev)
        padded = jnp.concatenate([hidden, from_below], axis=1)
        return lax.conv_general_dilated(padded, weight, (2, 2), ((0, 0), (0, 1)), dimension_numbers=CONV_DIMS, preferred_element_type=jnp.float32)

    def conv_point(hidden, weight):
        return jnp.einsum("bhwc,cd->bhwd", hidden, weight, preferred_element_type=jnp.float32)

    def batch_norm(pre_act, params):
        norm_count = pre_act.shape[0] * pre_act.shape[1] * pre_act.shape[2] * groups
        part_sums = jnp.stack([jnp.sum(pre_act, axis=(0, 1, 2)), jnp.sum(pre_act * pre_act, axis=(0, 1, 2))])
        group_moments = lax.psum(part_sums, "sp") / norm_count
        chan_mean = group_moments[0]
        chan_var = group_moments[1] - chan_mean * chan_mean
        chan_scale = params[0] * lax.rsqrt(chan_var + NORM_EPS)
        return (pre_act - chan_mean) * chan_scale + params[1]

    def norm_relu(pre_act, params):
        return jax.nn.relu(batch_norm(pre_act, params)).astype(jnp.bfloat16)

    def forward(images, w_a, bn_a, w_down, bn_down, w_in, bn_in, w_mid, bn_mid, w_out, bn_out):
        hidden = images
        for layer_num in range(w_a.shape[0]):
            hidden = norm_relu(conv_same(hidden, w_a[layer_num]), bn_a[layer_num])
        hidden = norm_relu(conv_down(hidden, w_down), bn_down)
        for block_num in range(w_in.shape[0]):
            branch = norm_relu(conv_point(hidden, w_in[block_num]), bn_in[block_num])
            branch = norm_relu(conv_same(branch, w_mid[block_num]), bn_mid[block_num])
            summed = batch_norm(conv_point(branch, w_out[block_num]), bn_out[block_num]) + hidden
            hidden = jax.nn.relu(summed).astype(jnp.bfloat16)
        return hidden

    act_spec = P("dp", "sp", None, None)
    return jax.shard_map(forward, mesh=mesh, in_specs=(act_spec,) + (P(),) * 10, out_specs=act_spec, check_vma=False)
```

profile of v0, /device:TPU:97, one launch (start us, length us, event | category | flops | bytes accessed | tf_op | source)
XLA Modules:
  0.0 795.5 jit_solution(16889031212661378188)
XLA Ops:
  8.6 9.7 %collective-permute-done = bf16[32,1,512,32]{2,3,1,0:T(8,128)(2,1)S(1)} collective-permute-done((bf16[32,1,512,32]{2,3,1,0:T(8,128)(2,1)S(1)}, bf16[32,1,512,32]{2,3,1,0:T(8,128)(2,1)S(1)}, u32[]{:S(2)}, u32[]{:S(2)}) %collective-permute-start) | collective-permute-done | bytes 1048608 | tf_op jit(solution)/shard_map/ppermute | solution.py:16
  24.9 23.3 %copy.45 = bf16[32,4,512,32]{3,0,2,1:T(8,128)(2,1)} copy(bf16[32,4,512,32]{2,3,1,0:T(8,128)(2,1)} %pad_maximum_fusion) | data formatting | bytes 8388608 | tf_op jit(solution)/shard_map/concatenate | solution.py:18
  48.2 26.9 %fusion.92 = (f32[32]{0:T(128)S(1)}, f32[32]{0:T(128)S(1)}, f32[32,2,512,32]{3,0,2,1:T(8,128)}) fusion(bf16[32,4,512,32]{3,0,2,1:T(8,128)(2,1)} %copy.45, bf16[1,3,3,32,32]{4,3,2,1,0:T(8,128)(2,1)S(1)} %copy-done.12), kind=kOutput, calls=%fused_computation.176 | convolution fusion | flops 606339072 | bytes 8407296 | tf_op jit(solution)/shard_map/conv_general_dilated | solution.py:19
  75.2 48.6 %psum.77 = f32[2,32]{1,0:T(2,128)S(1)} all-reduce(f32[2,32]{1,0:T(2,128)S(1)} %pad_maximum_fusion.4), channel_id=1, replica_groups=mesh['dp'=1,'sp'=32] {'sp'}, use_global_device_ids=true, to_apply=%region_2.0 | all-reduce | flops 64 | bytes 512 | tf_op jit(solution)/shard_map/psum | solution.py:32
  144.2 13.5 %collective-permute-done.2 = bf16[32,1,512,32]{2,3,1,0:T(8,128)(2,1)S(1)} collective-permute-done((bf16[32,1,512,32]{2,3,1,0:T(8,128)(2,1)S(1)}, bf16[32,1,512,32]{2,3,1,0:T(8,128)(2,1)S(1)}, u32[]{:S(2)}, u32[]{:S(2)}) %collective-permute-start.2) | collective-permute-done | bytes 1048608 | tf_op jit(solution)/shard_map/ppermute | solution.py:22
  164.2 11.0 %fusion.99 = (f32[128]{0:T(128)S(1)}, f32[128]{0:T(128)S(1)}, f32[32,1,256,128]{3,0,2,1:T(8,128)}) fusion(bf16[3,3,32,128]{3,2,1,0:T(8,128)(2,1)S(1)} %copy-done, bf16[32,1,512,32]{3,0,2,1:T(8,128)(2,1)} %copy.47, bf16[32,2,512,32]{3,0,2,1:T(8,128)(2,1)} %copy-done.3), kind=kOutput, calls=%fused_computation.183 | convolution fusion | flops 612630272 | bytes 7414784 | tf_op jit(solution)/shard_map/conv_general_dilated | solution.py:24
  175.1 46.7 %psum.78 = f32[2,128]{1,0:T(2,128)S(1)} all-reduce(f32[2,128]{1,0:T(2,128)S(1)} %pad_maximum_fusion.5), channel_id=1, replica_groups=mesh['dp'=1,'sp'=32] {'sp'}, use_global_device_ids=true, to_apply=%region_5.6 | all-reduce | flops 256 | bytes 2048 | tf_op jit(solution)/shard_map/psum | solution.py:32
  226.1 44.8 %psum.79 = f32[2,64]{1,0:T(2,128)S(1)} all-reduce(f32[2,64]{1,0:T(2,128)S(1)} %pad_maximum_fusion.6), channel_id=1, replica_groups=mesh['dp'=1,'sp'=32] {'sp'}, use_global_device_ids=true, to_apply=%region_8.9 | all-reduce | flops 128 | bytes 1024 | tf_op jit(solution)/shard_map/psum | solution.py:32
  276.8 9.7 %collective-permute-done.3 = bf16[32,1,256,64]{2,3,0,1:T(8,128)(2,1)S(1)} collective-permute-done((bf16[32,1,256,64]{2,3,0,1:T(8,128)(2,1)S(1)}, bf16[32,1,256,64]{2,3,0,1:T(8,128)(2,1)S(1)}, u32[]{:S(2)}, u32[]{:S(2)}) %collective-permute-start.3) | collective-permute-done | bytes 1048608 | tf_op jit(solution)/shard_map/ppermute | solution.py:16
  291.3 9.5 %copy.49 = bf16[32,3,256,64]{3,0,2,1:T(8,128)(2,1)} copy(bf16[32,3,256,64]{2,3,0,1:T(8,128)(2,1)S(1)} %pad_maximum_fusion.1) | data formatting | bytes 6291456 | tf_op jit(solution)/shard_map/concatenate | solution.py:18
  308.6 46.7 %psum.80 = f32[2,64]{1,0:T(2,128)S(1)} all-reduce(f32[2,64]{1,0:T(2,128)S(1)} %pad_maximum_fusion.7), channel_id=1, replica_groups=mesh['dp'=1,'sp'=32] {'sp'}, use_global_device_ids=true, to_apply=%region_11.12 | all-reduce | flops 128 | bytes 1024 | tf_op jit(solution)/shard_map/psum | solution.py:32
  361.6 44.8 %psum.81 = f32[2,128]{1,0:T(2,128)S(1)} all-reduce(f32[2,128]{1,0:T(2,128)S(1)} %pad_maximum_fusion.8), channel_id=1, replica_groups=mesh['dp'=1,'sp'=32] {'sp'}, use_global_device_ids=true, to_apply=%region_14.15 | all-reduce | flops 256 | bytes 2048 | tf_op jit(solution)/shard_map/psum | solution.py:32
  415.4 44.6 %psum.82 = f32[2,64]{1,0:T(2,128)S(1)} all-reduce(f32[2,64]{1,0:T(2,128)S(1)} %pad_maximum_fusion.9), channel_id=1, replica_groups=mesh['dp'=1,'sp'=32] {'sp'}, use_global_device_ids=true, to_apply=%region_17.18 | all-reduce | flops 128 | bytes 1024 | tf_op jit(solution)/shard_map/psum | solution.py:32
  465.7 9.7 %collective-permute-done.5 = bf16[32,1,256,64]{2,3,0,1:T(8,128)(2,1)S(1)} collective-permute-done((bf16[32,1,256,64]{2,3,0,1:T(8,128)(2,1)S(1)}, bf16[32,1,256,64]{2,3,0,1:T(8,128)(2,1)S(1)}, u32[]{:S(2)}, u32[]{:S(2)}) %collective-permute-start.5) | collective-permute-done | bytes 1048608 | tf_op jit(solution)/shard_map/ppermute | solution.py:16
  480.2 9.7 %copy.53 = bf16[32,3,256,64]{3,0,2,1:T(8,128)(2,1)} copy(bf16[32,3,256,64]{2,3,0,1:T(8,128)(2,1)S(1)} %pad_maximum_fusion.2) | data formatting | bytes 6291456 | tf_op jit(solution)/shard_map/concatenate | solution.py:18
  489.9 7.8 fusion.96
  497.8 46.5 %psum.83 = f32[2,64]{1,0:T(2,128)S(1)} all-reduce(f32[2,64]{1,0:T(2,128)S(1)} %pad_maximum_fusion.10), channel_id=1, replica_groups=mesh['dp'=1,'sp'=32] {'sp'}, use_global_device_ids=true, to_apply=%region_20.21 | all-reduce | flops 128 | bytes 1024 | tf_op jit(solution)/shard_map/psum | solution.py:32
  550.7 45.0 %psum.84 = f32[2,128]{1,0:T(2,128)S(1)} all-reduce(f32[2,128]{1,0:T(2,128)S(1)} %pad_maximum_fusion.11), channel_id=1, replica_groups=mesh['dp'=1,'sp'=32] {'sp'}, use_global_device_ids=true, to_apply=%region_23.24 | all-reduce | flops 256 | bytes 2048 | tf_op jit(solution)/shard_map/psum | solution.py:32
  603.9 44.6 %psum.85 = f32[2,64]{1,0:T(2,128)S(1)} all-reduce(f32[2,64]{1,0:T(2,128)S(1)} %pad_maximum_fusion.12), channel_id=1, replica_groups=mesh['dp'=1,'sp'=32] {'sp'}, use_global_device_ids=true, to_apply=%region_26.27 | all-reduce | flops 128 | bytes 1024 | tf_op jit(solution)/shard_map/psum | solution.py:32
  655.8 9.7 %collective-permute-done.7 = bf16[32,1,256,64]{2,3,0,1:T(8,128)(2,1)S(1)} collective-permute-done((bf16[32,1,256,64]{2,3,0,1:T(8,128)(2,1)S(1)}, bf16[32,1,256,64]{2,3,0,1:T(8,128)(2,1)S(1)}, u32[]{:S(2)}, u32[]{:S(2)}) %collective-permute-start.7) | collective-permute-done | bytes 1048608 | tf_op jit(solution)/shard_map/ppermute | solution.py:16
  672.0 10.6 %copy.57 = bf16[32,3,256,64]{3,0,2,1:T(8,128)(2,1)} copy(bf16[32,3,256,64]{2,3,0,1:T(8,128)(2,1)} %pad_maximum_fusion.3) | data formatting | bytes 6291456 | tf_op jit(solution)/shard_map/concatenate | solution.py:18
  682.6 7.8 fusion.94
  690.5 46.5 %psum.86 = f32[2,64]{1,0:T(2,128)S(1)} all-reduce(f32[2,64]{1,0:T(2,128)S(1)} %pad_maximum_fusion.13), channel_id=1, replica_groups=mesh['dp'=1,'sp'=32] {'sp'}, use_global_device_ids=true, to_apply=%region_29.30 | all-reduce | flops 128 | bytes 1024 | tf_op jit(solution)/shard_map/psum | solution.py:32
  743.4 44.9 %psum.87 = f32[2,128]{1,0:T(2,128)S(1)} all-reduce(f32[2,128]{1,0:T(2,128)S(1)} %pad_maximum_fusion.14), channel_id=1, replica_groups=mesh['dp'=1,'sp'=32] {'sp'}, use_global_device_ids=true, to_apply=%region_32.33 | all-reduce | flops 256 | bytes 2048 | tf_op jit(solution)/shard_map/psum | solution.py:32
  (115 shorter events, 132.0 us)
Async XLA Ops:
  0.0 164.2 %copy-start = (bf16[3,3,32,128]{3,2,1,0:T(8,128)(2,1)S(1)}, bf16[3,3,32,128]{3,2,1,0:T(8,128)(2,1)}, u32[]{:S(2)}) copy-start(bf16[3,3,32,128]{3,2,1,0:T(8,128)(2,1)} %param.14) | copy-start | bytes 221188
  0.0 22.7 %copy-start.4 = (bf16[32,2,512,32]{2,3,1,0:T(8,128)(2,1)S(1)}, bf16[32,2,512,32]{2,3,1,0:T(8,128)(2,1)}, u32[]{:S(2)}) copy-start(bf16[32,2,512,32]{2,3,1,0:T(8,128)(2,1)} %param.11) | copy-start | bytes 6291460
  0.0 8.5 %copy-start.10 = (f32[1,2,32]{2,1,0:T(2,128)S(1)}, f32[1,2,32]{2,1,0:T(2,128)}, u32[]{:S(2)}) copy-start(f32[1,2,32]{2,1,0:T(2,128)} %param.13) | copy-start | bytes 772
  2.0 16.3 %collective-permute-start = (bf16[32,1,512,32]{2,3,1,0:T(8,128)(2,1)S(1)}, bf16[32,1,512,32]{2,3,1,0:T(8,128)(2,1)S(1)}, u32[]{:S(2)}, u32[]{:S(2)}) collective-permute-start(bf16[32,1,512,32]{2,3,1,0:T(8,128)(2,1)S(1)} %get-tuple-element.27), channel_id=1, source_target_pairs={{0,1},{1,2},{2,3},{3,4},{4,5},{5,6},{6,7},{7,8},{8,9},{9,10},{10,1... | collective-permute-start | bytes 3145736 | tf_op jit(solution)/shard_map/ppermute | solution.py:16
  6.6 16.1 %collective-permute-start.1 = (bf16[32,1,512,32]{2,3,1,0:T(8,128)(2,1)S(1)}, bf16[32,1,512,32]{2,3,1,0:T(8,128)(2,1)S(1)}, u32[]{:S(2)}, u32[]{:S(2)}) collective-permute-start(bf16[32,1,512,32]{2,3,1,0:T(8,128)(2,1)S(1)} %get-tuple-element.28), channel_id=1, source_target_pairs={{1,0},{2,1},{3,2},{4,3},{5,4},{6,5},{7,6},{8,7},{9,8},{10,9},{11,1... | collective-permute-start | bytes 3145736 | tf_op jit(solution)/shard_map/ppermute | solution.py:17
  24.9 23.4 %copy-start.12 = (bf16[1,3,3,32,32]{4,3,2,1,0:T(8,128)(2,1)S(1)}, bf16[1,3,3,32,32]{4,3,2,1,0:T(8,128)(2,1)}, u32[]{:S(2)}) copy-start(bf16[1,3,3,32,32]{4,3,2,1,0:T(8,128)(2,1)} %param.12) | copy-start | bytes 55300
  131.2 3.2 copy-start.3
  137.1 7.1 copy-start.11
  137.1 7.1 copy-start.7
  141.6 16.1 %collective-permute-start.2 = (bf16[32,1,512,32]{2,3,1,0:T(8,128)(2,1)S(1)}, bf16[32,1,512,32]{2,3,1,0:T(8,128)(2,1)S(1)}, u32[]{:S(2)}, u32[]{:S(2)}) collective-permute-start(bf16[32,1,512,32]{2,3,1,0:T(8,128)(2,1)S(1)} %copy.46), channel_id=1, source_target_pairs={{1,0},{2,1},{3,2},{4,3},{5,4},{6,5},{7,6},{8,7},{9,8},{10,9},{11,1... | collective-permute-start | bytes 3145736 | tf_op jit(solution)/shard_map/ppermute | solution.py:22
  175.1 49.6 %copy-start.5 = (bf16[3,128,64]{1,2,0:T(8,128)(2,1)S(1)}, bf16[3,128,64]{1,2,0:T(8,128)(2,1)}, u32[]{:S(2)}) copy-start(bf16[3,128,64]{1,2,0:T(8,128)(2,1)} %param.16) | copy-start | bytes 147460
  224.8 52.0 %copy-start.8 = (f32[3,2,64]{2,1,0:T(2,128)S(1)}, f32[3,2,64]{2,1,0:T(2,128)}, u32[]{:S(2)}) copy-start(f32[3,2,64]{2,1,0:T(2,128)} %param.19) | copy-start | bytes 4612
  224.8 52.0 %copy-start.9 = (f32[3,2,128]{2,1,0:T(2,128)S(1)}, f32[3,2,128]{2,1,0:T(2,128)}, u32[]{:S(2)}) copy-start(f32[3,2,128]{2,1,0:T(2,128)} %param.21) | copy-start | bytes 9220
  271.4 15.1 %collective-permute-start.3 = (bf16[32,1,256,64]{2,3,0,1:T(8,128)(2,1)S(1)}, bf16[32,1,256,64]{2,3,0,1:T(8,128)(2,1)S(1)}, u32[]{:S(2)}, u32[]{:S(2)}) collective-permute-start(bf16[32,1,256,64]{2,3,0,1:T(8,128)(2,1)S(1)} %fusion.31), channel_id=1, source_target_pairs={{0,1},{1,2},{2,3},{3,4},{4,5},{5,6},{6,7},{7,8},{8,9},{9,10},{10,1... | collective-permute-start | bytes 3145736 | tf_op jit(solution)/shard_map/ppermute | solution.py:16
  274.8 16.1 %collective-permute-start.4 = (bf16[32,1,256,64]{2,3,0,1:T(8,128)(2,1)S(1)}, bf16[32,1,256,64]{2,3,0,1:T(8,128)(2,1)S(1)}, u32[]{:S(2)}, u32[]{:S(2)}) collective-permute-start(bf16[32,1,256,64]{2,3,0,1:T(8,128)(2,1)S(1)} %fusion.31), channel_id=1, source_target_pairs={{1,0},{2,1},{3,2},{4,3},{5,4},{6,5},{7,6},{8,7},{9,8},{10,9},{11,1... | collective-permute-start | bytes 3145736 | tf_op jit(solution)/shard_map/ppermute | solution.py:17
  308.5 49.6 %copy-start.6 = (bf16[3,64,128]{2,1,0:T(8,128)(2,1)S(1)}, bf16[3,64,128]{2,1,0:T(8,128)(2,1)}, u32[]{:S(2)}) copy-start(bf16[3,64,128]{2,1,0:T(8,128)(2,1)} %param.20) | copy-start | bytes 147460
  412.7 1.3 copy-start.2
  460.5 14.9 %collective-permute-start.5 = (bf16[32,1,256,64]{2,3,0,1:T(8,128)(2,1)S(1)}, bf16[32,1,256,64]{2,3,0,1:T(8,128)(2,1)S(1)}, u32[]{:S(2)}, u32[]{:S(2)}) collective-permute-start(bf16[32,1,256,64]{2,3,0,1:T(8,128)(2,1)S(1)} %fusion.32), channel_id=1, source_target_pairs={{0,1},{1,2},{2,3},{3,4},{4,5},{5,6},{6,7},{7,8},{8,9},{9,10},{10,1... | collective-permute-start | bytes 3145736 | tf_op jit(solution)/shard_map/ppermute | solution.py:16
  463.7 16.1 %collective-permute-start.6 = (bf16[32,1,256,64]{2,3,0,1:T(8,128)(2,1)S(1)}, bf16[32,1,256,64]{2,3,0,1:T(8,128)(2,1)S(1)}, u32[]{:S(2)}, u32[]{:S(2)}) collective-permute-start(bf16[32,1,256,64]{2,3,0,1:T(8,128)(2,1)S(1)} %fusion.32), channel_id=1, source_target_pairs={{1,0},{2,1},{3,2},{4,3},{5,4},{6,5},{7,6},{8,7},{9,8},{10,9},{11,1... | collective-permute-start | bytes 3145736 | tf_op jit(solution)/shard_map/ppermute | solution.py:17
  650.5 14.9 %collective-permute-start.7 = (bf16[32,1,256,64]{2,3,0,1:T(8,128)(2,1)S(1)}, bf16[32,1,256,64]{2,3,0,1:T(8,128)(2,1)S(1)}, u32[]{:S(2)}, u32[]{:S(2)}) collective-permute-start(bf16[32,1,256,64]{2,3,0,1:T(8,128)(2,1)S(1)} %fusion.33), channel_id=1, source_target_pairs={{0,1},{1,2},{2,3},{3,4},{4,5},{5,6},{6,7},{7,8},{8,9},{9,10},{10,1... | collective-permute-start | bytes 3145736 | tf_op jit(solution)/shard_map/ppermute | solution.py:16
  653.8 16.1 %collective-permute-start.8 = (bf16[32,1,256,64]{2,3,0,1:T(8,128)(2,1)S(1)}, bf16[32,1,256,64]{2,3,0,1:T(8,128)(2,1)S(1)}, u32[]{:S(2)}, u32[]{:S(2)}) collective-permute-start(bf16[32,1,256,64]{2,3,0,1:T(8,128)(2,1)S(1)} %fusion.33), channel_id=1, source_target_pairs={{1,0},{2,1},{3,2},{4,3},{5,4},{6,5},{7,6},{8,7},{9,8},{10,9},{11,1... | collective-permute-start | bytes 3145736 | tf_op jit(solution)/shard_map/ppermute | solution.py:17
  788.3 7.0 copy-start.1
where the time goes:
time: 800 us; the launch traced here: 796 us
  blocking collectives  504 us (63%)
  matrix products  76.9 us (10%)
  local copies, waits for them, and re-layouts  75.5 us (9%)
  waiting for transfers between devices  70.2 us (9%)
  other arithmetic  43.7 us (5%)
  starting transfers between devices  24.9 us (3%)
    psum x11, blocking collectives, batch_norm(): group_moments = lax.psum(part_sums, 'sp') / norm_count  504 us
    concatenate x4, local copies, waits for them, and re-layouts, conv_same(): padded = jnp.concatenate([from_above, hidden, from_below], axis=1)  53.2 us
    conv_general_dilated x4, matrix products, conv_same(): lax.conv_general_dilated(padded, weight, (1, 1), ((0, 0), (1, 1)), dimens...  50.3 us
    ppermute x4, waiting for transfers between devices, conv_same(): from_above = lax.ppermute(hidden[:, -1:], 'sp', to_next)  38.9 us
    ppermute x4, waiting for transfers between devices, conv_same(): from_below = lax.ppermute(hidden[:, :1], 'sp', to_prev)  17.8 us
    convert_element_type x3, other arithmetic, forward(): hidden = jax.nn.relu(summed).astype(jnp.bfloat16)  16.6 us
  transfers between devices with their start and end apart: 9, of which 9 were waited for; matrix products, arithmetic and copies ran while one was open for 0% of the time, Pallas kernels for 0%

commit v1 on v0

v1 whole, which is shorter than its diff:
```python
import functools

import jax
import jax.numpy as jnp
import numpy as np
from jax import lax
from jax.experimental import pallas as pl
from jax.experimental.pallas import tpu as pltpu
from jax.sharding import PartitionSpec as P

NORM_EPS = 1e-5
MESH = pl.DeviceIdType.MESH
LANES = 128
F32 = jnp.float32
BF16 = jnp.bfloat16


def place_taps(taps, index):
    count, ci, co = taps.shape
    rows, cols = index.shape
    pick = np.zeros((rows, cols, count), np.float32)
    for r in range(rows):
        for c in range(cols):
            if index[r, c] < count:
                pick[r, c, index[r, c]] = 1.0
    blocks = jnp.einsum("rct,tio->rico", jnp.asarray(pick, BF16), taps, preferred_element_type=F32)
    return blocks.astype(BF16).reshape(rows * ci, cols * co)


def stage_a_index(halo):
    index = np.full((8, 16), 9, np.int64)
    for pi in range(2):
        for a in range(2):
            for ri in range(2):
                for shift in range(2):
                    for ro in range(2):
                        for po in range(2):
                            if halo:
                                if ri != ro:
                                    continue
                                ky = 0 if ri == 0 else 2
                            else:
                                ky = ri - ro + 1
                            if shift == 0:
                                kx = pi - po + 1
                            elif pi != po:
                                kx = 0 if pi == 1 else 2
                            else:
                                continue
                            index[(pi * 2 + a) * 2 + ri, ((shift * 2 + a) * 2 + ro) * 2 + po] = ky * 3 + kx
    return index


def down_own_index():
    index = np.full((4, 2), 9, np.int64)
    for row in range(2):
        for par in range(2):
            index[row * 2 + par, 0] = row * 3 + par
        index[row * 2, 1] = row * 3 + 2
    return index


def down_halo_index():
    index = np.full((4, 4), 9, np.int64)
    for a in range(2):
        for par in range(2):
            index[a * 2 + par, a * 2] = 6 + par
        index[a * 2, a * 2 + 1] = 8
    return index


def mid_index():
    index = np.full((6, 6), 9, np.int64)
    for src, ky in enumerate((1, 0, 2)):
        for kx in range(3):
            for a in range(2):
                index[src * 2 + a, kx * 2 + a] = ky * 3 + kx
    return index


def kernel(
    n, img_hbm, wao_ref, wah_ref, wdo_ref, wdh_ref, win_ref, wmid_ref, wout_ref, bn_ref, out_hbm,
    ximg, xabove, xbelow, tscr, za, rsend, rrecv, zd, h, zi, u2, habove, hbelow, zm, zo, stats, recv,
    img_sem, isend_sem, irecv_sem, rsend_sem, rrecv_sem, hsend_sem, hrecv_sem, ssem, rsem, out_sem,
):
    me = lax.axis_index("sp")
    nxt, prv = me + 1, me - 1
    has_next, has_prev = me < n - 1, me > 0
    pairs, chunks = ximg.shape[1], isend_sem.shape[1]
    per = pairs // chunks
    half_w = tscr.shape[0] // 2
    full_w = tscr.shape[0]
    rows_all = lax.axis_size("sp")
    count_a = float(2 * pairs * 2 * full_w) * rows_all
    count_b = float(2 * pairs * half_w) * rows_all

    local_img = [
        pltpu.make_async_copy(img_hbm.at[:, pl.ds(c * per, per)], ximg.at[:, pl.ds(c * per, per)], img_sem.at[c])
        for c in range(chunks)
    ]
    for copy in local_img:
        copy.start()

    xabove[...] = jnp.zeros_like(xabove)
    xbelow[...] = jnp.zeros_like(xbelow)

    @pl.when(me == n - 1)
    def _():
        rrecv[...] = jnp.zeros_like(rrecv)
        hbelow[...] = jnp.zeros_like(hbelow)

    @pl.when(me == 0)
    def _():
        habove[...] = jnp.zeros_like(habove)

    barrier = pltpu.get_barrier_semaphore()

    def greet(d, carry):
        pl.semaphore_signal(barrier, inc=1, device_id={"sp": lax.rem(me + d, n)}, device_id_type=MESH)
        return carry

    lax.fori_loop(1, n, greet, 0)
    pl.semaphore_wait(barrier, n - 1)

    def to_dev(src, dst, send_sem, recv_sem, dev):
        return pltpu.make_async_remote_copy(
            src_ref=src, dst_ref=dst, send_sem=send_sem, recv_sem=recv_sem, device_id={"sp": dev}, device_id_type=MESH
        )

    def img_down(c):
        part = pl.ds(c * per, per)
        return to_dev(img_hbm.at[:, part, 1], xabove.at[:, part], isend_sem.at[0, c], irecv_sem.at[0, c], nxt)

    def img_up(c):
        part = pl.ds(c * per, per)
        return to_dev(img_hbm.at[:, part, 0], xbelow.at[:, part], isend_sem.at[1, c], irecv_sem.at[1, c], prv)

    for c in range(chunks):
        @pl.when(has_next)
        def _():
            img_down(c).start()

        @pl.when(has_prev)
        def _():
            img_up(c).start()

    def shift_down(y):
        row = lax.broadcasted_iota(jnp.int32, y.shape, 0)
        return jnp.where(row == 0, 0.0, pltpu.roll(y, 1, 0))

    def shift_up(y):
        row = lax.broadcasted_iota(jnp.int32, y.shape, 0)
        return jnp.where(row == y.shape[0] - 1, 0.0, pltpu.roll(y, y.shape[0] - 1, 0))

    def add_stats(acc, z):
        blocks = z.reshape(z.shape[0] // 8, 8, LANES)
        return acc[0] + jnp.sum(blocks, axis=0), acc[1] + jnp.sum(blocks * blocks, axis=0)

    zero_acc = (jnp.zeros((8, LANES), F32), jnp.zeros((8, LANES), F32))

    def group_stats(k, acc, group):
        def fold(v):
            width = group
            while width < LANES:
                v = v + pltpu.roll(v, width, 1)
                width *= 2
            return jnp.sum(v, axis=0, keepdims=True)

        mine = jnp.concatenate([fold(acc[0]), fold(acc[1])], axis=0)
        stats[k] = mine

        def send(d, carry):
            to_dev(stats.at[k], recv.at[k, d - 1], ssem.at[k], rsem.at[k], lax.rem(me + d, n)).start()
            return carry

        lax.fori_loop(1, n, send, 0)
        to_dev(recv.at[k], recv.at[k], ssem.at[k], rsem.at[k], me).wait_recv()
        return mine + jnp.sum(recv[k], axis=0)

    def norm_of(k, total, count):
        moments = total * (1.0 / count)
        mean = moments[0:1]
        var = moments[1:2] - mean * mean
        scale = bn_ref[k, 0:1] * lax.rsqrt(var + NORM_EPS)
        return mean, scale, bn_ref[k, 1:2]

    def bn(z, norm):
        mean, scale, shift = norm
        return (z - mean) * scale + shift

    lane2 = lax.broadcasted_iota(jnp.int32, (half_w, 2 * LANES), 1)
    even_lane = lax.rem(lane2 // 32, 2) == 0

    def stage_a_part(x, w_ref):
        tscr[...] = x.astype(F32).T
        lhs = jnp.concatenate(
            [tscr[pl.ds(0, half_w, stride=2), :], tscr[pl.ds(1, half_w, stride=2), :]], axis=1
        ).astype(BF16)
        y = jnp.dot(lhs, w_ref[...], preferred_element_type=F32)
        cross = y[:, 2 * LANES:]
        return y[:, : 2 * LANES] + jnp.where(even_lane, shift_down(cross), shift_up(cross))

    for c in range(chunks):
        local_img[c].wait()

        def own_a(q, carry):
            x = jnp.concatenate(
                [ximg[0, q].reshape(2 * 32, full_w), ximg[1, q].reshape(2 * 32, full_w)], axis=0
            )
            z = stage_a_part(x, wao_ref)
            za[0, q] = z[:, :LANES]
            za[1, q] = z[:, LANES:]
            return carry

        lax.fori_loop(c * per, (c + 1) * per, own_a, 0)

    acc = zero_acc
    for c in range(chunks):
        @pl.when(has_prev)
        def _():
            img_down(c).wait_recv()

        @pl.when(has_next)
        def _():
            img_up(c).wait_recv()

        def halo_a(q, acc):
            x = jnp.concatenate([xabove[0, q], xbelow[0, q], xabove[1, q], xbelow[1, q]], axis=0)
            z = stage_a_part(x, wah_ref)
            z0 = za[0, q] + z[:, :LANES]
            z1 = za[1, q] + z[:, LANES:]
            za[0, q] = z0
            za[1, q] = z1
            return add_stats(add_stats(acc, z0), z1)

        acc = lax.fori_loop(c * per, (c + 1) * per, halo_a, acc)
    norm = norm_of(0, group_stats(0, acc, 32), count_a)

    lane1 = lax.broadcasted_iota(jnp.int32, (half_w, LANES), 1)
    low_lane = lane1 < 64

    def row_up(c):
        part = pl.ds(c * per, per)
        return to_dev(rsend.at[part], rrecv.at[part], rsend_sem.at[c], rrecv_sem.at[c], prv)

    for c in range(chunks):
        def own_down(q, carry):
            t0 = jnp.maximum(bn(za[0, q], norm), 0.0)
            t1 = jnp.maximum(bn(za[1, q], norm), 0.0)
            rsend[q] = jnp.where(low_lane, t0, pltpu.roll(t1, 64, 1)).astype(BF16)
            for a, t in enumerate((t0, t1)):
                y = jnp.dot(t.astype(BF16), wdo_ref[...], preferred_element_type=F32)
                zd[a, q] = y[:, :LANES] + shift_up(y[:, LANES:])
            return carry

        lax.fori_loop(c * per, (c + 1) * per, own_down, 0)

        @pl.when(has_prev)
        def _():
            row_up(c).start()

    acc = zero_acc
    for c in range(chunks):
        @pl.when(has_next)
        def _():
            row_up(c).wait_recv()

        def halo_down(q, acc):
            y = jnp.dot(rrecv[q], wdh_ref[...], preferred_element_type=F32)
            for a in range(2):
                lo = 2 * a * LANES
                z = zd[a, q] + y[:, lo:lo + LANES] + shift_up(y[:, lo + LANES:lo + 2 * LANES])
                zd[a, q] = z
                acc = add_stats(acc, z)
            return acc

        acc = lax.fori_loop(c * per, (c + 1) * per, halo_down, acc)
    norm = norm_of(1, group_stats(1, acc, LANES), count_b)

    blocks = win_ref.shape[0]

    def mid_down(j, c):
        part = pl.ds(c * per, per)
        return to_dev(u2.at[j, part], habove.at[j, part], hsend_sem.at[j, 0, c], hrecv_sem.at[j, 0, c], nxt)

    def mid_up(j, c):
        part = pl.ds(c * per, per)
        return to_dev(u2.at[j, part], hbelow.at[j, part], hsend_sem.at[j, 1, c], hrecv_sem.at[j, 1, c], prv)

    for j in range(blocks):
        def layer_in(q, acc):
            parts = []
            for a in range(2):
                if j == 0:
                    t = bn(zd[a, q], norm)
                else:
                    t = bn(zo[a, q], norm) + h[a, q].astype(F32)
                t = jnp.maximum(t, 0.0).astype(BF16)
                h[a, q] = t
                parts.append(t)
            z = jnp.dot(jnp.concatenate(parts, axis=1), win_ref[j], preferred_element_type=F32)
            zi[q] = z
            return add_stats(acc, z)

        acc = lax.fori_loop(0, pairs, layer_in, zero_acc)
        norm = norm_of(2 + 3 * j, group_stats(2 + 3 * j, acc, 64), count_b)

        for c in range(chunks):
            def act_in(q, carry):
                u2[j, q] = jnp.maximum(bn(zi[q], norm), 0.0).astype(BF16)
                return carry

            lax.fori_loop(c * per, (c + 1) * per, act_in, 0)

            @pl.when(has_next)
            def _():
                mid_down(j, c).start()

            @pl.when(has_prev)
            def _():
                mid_up(j, c).start()

        acc = zero_acc
        for c in range(chunks):
            @pl.when(has_prev)
            def _():
                mid_down(j, c).wait_recv()

            @pl.when(has_next)
            def _():
                mid_up(j, c).wait_recv()

            def layer_mid(q, acc):
                lhs = jnp.concatenate([u2[j, q], habove[j, q], hbelow[j, q]], axis=1)
                y = jnp.dot(lhs, wmid_ref[j], preferred_element_type=F32)
                z = shift_down(y[:, :LANES]) + y[:, LANES:2 * LANES] + shift_up(y[:, 2 * LANES:])
                zm[q] = z
                return add_stats(acc, z)

            acc = lax.fori_loop(c * per, (c + 1) * per, layer_mid, acc)
        norm = norm_of(3 + 3 * j, group_stats(3 + 3 * j, acc, 64), count_b)

        def layer_out(q, acc):
            u = jnp.maximum(bn(zm[q], norm), 0.0).astype(BF16)
            y = jnp.dot(u, wout_ref[j], preferred_element_type=F32)
            for a in range(2):
                z = y[:, a * LANES:(a + 1) * LANES]
                zo[a, q] = z
                acc = add_stats(acc, z)
            return acc

        acc = lax.fori_loop(0, pairs, layer_out, zero_acc)
        norm = norm_of(4 + 3 * j, group_stats(4 + 3 * j, acc, LANES), count_b)

    def store(c):
        part = pl.ds(c * per, per)
        return pltpu.make_async_copy(h.at[:, part], out_hbm.at[:, part], out_sem.at[c])

    for c in range(chunks):
        def final(q, carry):
            for a in range(2):
                h[a, q] = jnp.maximum(bn(zo[a, q], norm) + h[a, q].astype(F32), 0.0).astype(BF16)
            return carry

        lax.fori_loop(c * per, (c + 1) * per, final, 0)
        store(c).start()

    for k in range(stats.shape[0]):
        to_dev(recv.at[k], recv.at[k], ssem.at[k], rsem.at[k], me).wait_send()

    @pl.when(has_next)
    def _():
        for c in range(chunks):
            img_down(c).wait_send()
            for j in range(blocks):
                mid_down(j, c).wait_send()

    @pl.when(has_prev)
    def _():
        for c in range(chunks):
            img_up(c).wait_send()
            row_up(c).wait_send()
            for j in range(blocks):
                mid_up(j, c).wait_send()

    for c in range(chunks):
        store(c).wait()


def solution(mesh):
    n = mesh.shape["sp"]

    def forward(images, w_a, bn_a, w_down, bn_down, w_in, bn_in, w_mid, bn_mid, w_out, bn_out):
        count, rows, width, chan_a = images.shape
        pairs, half_w = count // 2, width // 2
        blocks = w_in.shape[0]
        chunks = min(8, pairs)
        img = jnp.transpose(images, (0, 1, 3, 2)).reshape(2, pairs, rows, chan_a, width)
        taps_a = w_a[0].reshape(9, chan_a, chan_a)
        wao = place_taps(taps_a, stage_a_index(False))
        wah = place_taps(taps_a, stage_a_index(True))
        taps_d = w_down.reshape(9, chan_a, LANES)
        wdo = place_taps(taps_d, down_own_index())
        wdh = place_taps(taps_d, down_halo_index())
        eye = np.array([[0, 1], [1, 0]], np.int64)
        win = jnp.stack([place_taps(w_in[j][None], eye) for j in range(blocks)])
        wmid = jnp.stack([place_taps(w_mid[j].reshape(9, 64, 64), mid_index()) for j in range(blocks)])
        wout = jnp.stack([place_taps(w_out[j][None], eye) for j in range(blocks)])
        layers = [jnp.tile(bn_a[0], (1, 4)), bn_down]
        for j in range(blocks):
            layers += [jnp.tile(bn_in[j], (1, 2)), jnp.tile(bn_mid[j], (1, 2)), bn_out[j]]
        bn_all = jnp.stack(layers)
        steps = len(layers)

        vmem = pl.BlockSpec(memory_space=pltpu.VMEM)
        anyspace = pl.BlockSpec(memory_space=pl.ANY)
        dma = pltpu.SemaphoreType.DMA
        out = pl.pallas_call(
            functools.partial(kernel, n),
            out_shape=jax.ShapeDtypeStruct((2, pairs, half_w, LANES), BF16),
            in_specs=[anyspace] + [vmem] * 8,
            out_specs=anyspace,
            scratch_shapes=[
                pltpu.VMEM((2, pairs, rows, chan_a, width), BF16),
                pltpu.VMEM((2, pairs, chan_a, width), BF16),
                pltpu.VMEM((2, pairs, chan_a, width), BF16),
                pltpu.VMEM((width, LANES), F32),
                pltpu.VMEM((2, pairs, half_w, LANES), F32),
                pltpu.VMEM((pairs, half_w, LANES), BF16),
                pltpu.VMEM((pairs, half_w, LANES), BF16),
                pltpu.VMEM((2, pairs, half_w, LANES), F32),
                pltpu.VMEM((2, pairs, half_w, LANES), BF16),
                pltpu.VMEM((pairs, half_w, LANES), F32),
                pltpu.VMEM((blocks, pairs, half_w, LANES), BF16),
                pltpu.VMEM((blocks, pairs, half_w, LANES), BF16),
                pltpu.VMEM((blocks, pairs, half_w, LANES), BF16),
                pltpu.VMEM((pairs, half_w, LANES), F32),
                pltpu.VMEM((2, pairs, half_w, LANES), F32),
                pltpu.VMEM((steps, 2, LANES), F32),
                pltpu.VMEM((steps, n - 1, 2, LANES), F32),
                dma((chunks,)),
                dma((2, chunks)),
                dma((2, chunks)),
                dma((chunks,)),
                dma((chunks,)),
                dma((blocks, 2, chunks)),
                dma((blocks, 2, chunks)),
                dma((steps,)),
                dma((steps,)),
                dma((chunks,)),
            ],
            compiler_params=pltpu.CompilerParams(
                collective_id=0, has_side_effects=True, vmem_limit_bytes=60 * 1024 * 1024
            ),
        )(img, wao, wah, wdo, wdh, win, wmid, wout, bn_all)
        return out.reshape(count, rows // 2, half_w, LANES)

    act_spec = P("dp", "sp", None, None)
    return jax.shard_map(forward, mesh=mesh, in_specs=(act_spec,) + (P(),) * 10, out_specs=act_spec, check_vma=False)
```

time: 800 us -> 185 us (0.23)
  blocking collectives: 504 us -> 0 us
  Pallas kernels: 0 us -> 162 us
  matrix products: 76.9 us -> 3 us
  waiting for transfers between devices: 70.2 us -> 0 us
  local copies, waits for them, and re-layouts: 75.5 us -> 15.6 us
  other arithmetic: 43.7 us -> 4.29 us
  starting transfers between devices: 24.9 us -> 0 us
    psum x11 -> x0, blocking collectives: 504 us -> none  [batch_norm(): group_moments = lax.psum(part_sums, 'sp') / norm_count]
    pallas_call x0 -> x1, Pallas kernels: none -> 162 us  [forward(): pl.pallas_call(functools.partial(kernel, n), out_shape=jax.ShapeDtypeStru...]
    ppermute x9 -> x0, waiting for transfers between devices: 70.2 us -> none  [the longest x4 38.9 us: conv_same(): from_above = lax.ppermute(hidden[:, -1:], 'sp', to_next)]
    conv_general_dilated x5 -> x0, matrix products: 61.3 us -> none  [the longest x4 50.3 us: conv_same(): lax.conv_general_dilated(padded, weight, (1, 1), ((0, 0), (1, 1)), dimens...]
    concatenate x4 -> x0, local copies, waits for them, and re-layouts: 53.2 us -> none  [conv_same(): padded = jnp.concatenate([from_above, hidden, from_below], axis=1)]
    convert_element_type x7 -> x2, other arithmetic: 26.9 us -> 1.08 us  [place_taps(): return blocks.astype(BF16).reshape(rows * ci, cols * co)]
    ppermute x9 -> x0, starting transfers between devices: 24.9 us -> none  [the longest x4 14.5 us: conv_same(): from_above = lax.ppermute(hidden[:, -1:], 'sp', to_next)]
    dot_general x6 -> x7, matrix products: 15.6 us -> 3 us  [place_taps(): jnp.einsum('rct,tio->rico', jnp.asarray(pick, BF16), taps, preferred_elem...]
  transfers between devices with their start and end apart: 9 -> 0, of which waited for: 9 -> 0; matrix products, arithmetic and copies ran while one was open for 0% -> 0% of each run, Pallas kernels for 0% -> 0%
where the time goes in v1:
time: 185 us
  Pallas kernels  162 us (88%)
  local copies, waits for them, and re-layouts  15.6 us (8%)
  other arithmetic  4.29 us (2%)
  matrix products  3 us (2%)
    pallas_call x1, Pallas kernels, forward(): pl.pallas_call(functools.partial(kernel, n), out_shape=jax.ShapeDtypeStru...  162 us
    unnamed x33, local copies, waits for them, and re-layouts  6.6 us

profile of v1, /device:TPU:97, one launch (start us, length us, event | category | flops | bytes accessed | tf_op | source)
XLA Modules:
  0.0 184.8 jit_solution(8232357860096619981)
XLA Ops:
  0.0 0.8 slice_bitcast_fusion.1
  1.1 0.7 slice_bitcast_fusion
  2.0 0.7 tile.64
  2.8 0.7 constant_dynamic-update-slice_fusion.9
  3.5 0.7 constant_dynamic-update-slice_fusion.6
  4.2 0.7 constant_dynamic-update-slice_fusion.3
  4.9 0.7 constant_dynamic-update-slice_fusion.bn_ref
  5.6 1.1 fusion.5
  6.7 0.6 copy.88
  7.4 0.8 bitcast_convert_fusion.5
  8.1 0.9 fusion.20
  9.6 0.7 pad_maximum_fusion.1.win_ref
  10.6 0.7 pad_maximum_fusion.2.wout_ref
  11.5 0.7 copy.87
  12.6 0.5 stack_reshape.32
  13.4 0.5 stack_reshape.30
  14.2 0.5 stack_reshape.31
  14.7 1.0 pad_maximum_fusion.wmid_ref
  15.8 0.4 fusion.1
  16.2 1.7 reshape.125.wah_ref
  17.9 0.4 fusion
  18.3 1.7 reshape.124.wao_ref
  20.0 161.6 %shard_map.226 = bf16[2,16,256,128]{3,2,1,0:T(8,128)(2,1)} custom-call(bf16[2,16,2,32,512]{4,3,2,1,0:T(8,128)(2,1)} %bitcast.133, bf16[256,512]{1,0:T(8,128)(2,1)} %reshape.124.wao_ref, bf16[256,512]{1,0:T(8,128)(2,1)} %reshape.125.wah_ref, bf16[128,256]{1,0:T(8,128)(2,1)} %bitcast.143, bf16[128,512]{1,0:T(8,128)(2,1)} %bitcast.141, ...), custom_call_target="tpu_custom_call" | custom-call | tf_op jit(solution)/shard_map/pallas_call | solution.py:418
  181.7 3.1 %copy.100 = bf16[32,1,256,128]{3,2,1,0:T(8,128)(2,1)} copy(bf16[32,1,256,128]{3,2,1,0:T(8,128)(2,1)} %bitcast.132) | data formatting | bytes 4194304
  (57 shorter events, 2.8 us)
Async XLA Ops:
  0.0 10.3 %copy-start.9 = (f32[2,2]{1,0:T(2,128)S(1)}, f32[2,2]{1,0:T(2,128)}, u32[]{:S(2)}) copy-start(f32[2,2]{1,0:T(2,128)} %constant.26) | copy-start | bytes 52
  0.0 11.4 %copy-start.8 = (bf16[4,4,9,1]{2,1,3,0:T(4,128)(2,1)S(1)}, bf16[4,4,9,1]{2,1,3,0:T(4,128)(2,1)}, u32[]{:S(2)}) copy-start(bf16[4,4,9,1]{2,1,3,0:T(4,128)(2,1)} %constant.24) | copy-start | bytes 868
  0.0 10.3 %copy-start.4 = (bf16[3,64,128]{2,1,0:T(8,128)(2,1)S(1)}, bf16[3,64,128]{2,1,0:T(8,128)(2,1)}, u32[]{:S(2)}) copy-start(bf16[3,64,128]{2,1,0:T(8,128)(2,1)} %param.33) | copy-start | bytes 147460
  0.0 12.2 %copy-start.2 = (bf16[3,3,3,64,64]{4,3,2,1,0:T(8,128)(2,1)S(1)}, bf16[3,3,3,64,64]{4,3,2,1,0:T(8,128)(2,1)}, u32[]{:S(2)}) copy-start(bf16[3,3,3,64,64]{4,3,2,1,0:T(8,128)(2,1)} %param.31) | copy-start | bytes 663556
  0.0 11.3 %copy-start.1 = (bf16[3,3,32,128]{3,2,1,0:T(8,128)(2,1)S(1)}, bf16[3,3,32,128]{3,2,1,0:T(8,128)(2,1)}, u32[]{:S(2)}) copy-start(bf16[3,3,32,128]{3,2,1,0:T(8,128)(2,1)} %param.27) | copy-start | bytes 221188
  5.6 6.6 %copy-start.7 = (f32[11,2,128]{2,1,0:T(2,128)}, f32[11,2,128]{2,1,0:T(2,128)S(1)}, u32[]{:S(2)}) copy-start(f32[11,2,128]{2,1,0:T(2,128)S(1)} %constant_dynamic-update-slice_fusion.bn_ref) | copy-start | bytes 33796
  8.1 4.1 %copy-start.3 = (bf16[6,6,9,1]{2,1,3,0:T(8,128)(2,1)S(1)}, bf16[6,6,9,1]{2,1,3,0:T(8,128)(2,1)}, u32[]{:S(2)}) copy-start(bf16[6,6,9,1]{2,1,3,0:T(8,128)(2,1)} %constant.25) | copy-start | bytes 1948
  13.9 1.9 %copy-start = (bf16[1,3,3,32,32]{4,3,2,1,0:T(8,128)(2,1)S(1)}, bf16[1,3,3,32,32]{4,3,2,1,0:T(8,128)(2,1)}, u32[]{:S(2)}) copy-start(bf16[1,3,3,32,32]{4,3,2,1,0:T(8,128)(2,1)} %param.25) | copy-start | bytes 55300
  13.9 1.9 %copy-start.6 = (bf16[8,16,9,1]{2,1,3,0:T(8,128)(2,1)S(1)}, bf16[8,16,9,1]{2,1,3,0:T(8,128)(2,1)}, u32[]{:S(2)}) copy-start(bf16[8,16,9,1]{2,1,3,0:T(8,128)(2,1)} %constant.22) | copy-start | bytes 6916
  14.7 3.2 %copy-start.5 = (bf16[8,16,9,1]{2,1,3,0:T(8,128)(2,1)S(1)}, bf16[8,16,9,1]{2,1,3,0:T(8,128)(2,1)}, u32[]{:S(2)}) copy-start(bf16[8,16,9,1]{2,1,3,0:T(8,128)(2,1)} %constant.21) | copy-start | bytes 6916

commit v2 on v1

--- a/solution.py
+++ b/solution.py
@@ -2,7 +2,6 @@
 
 import jax
 import jax.numpy as jnp
-import numpy as np
 from jax import lax
 from jax.experimental import pallas as pl
 from jax.experimental.pallas import tpu as pltpu
@@ -15,71 +14,77 @@
 BF16 = jnp.bfloat16
 
 
-def place_taps(taps, index):
-    count, ci, co = taps.shape
-    rows, cols = index.shape
-    pick = np.zeros((rows, cols, count), np.float32)
-    for r in range(rows):
-        for c in range(cols):
-            if index[r, c] < count:
-                pick[r, c, index[r, c]] = 1.0
-    blocks = jnp.einsum("rct,tio->rico", jnp.asarray(pick, BF16), taps, preferred_element_type=F32)
-    return blocks.astype(BF16).reshape(rows * ci, cols * co)
-
-
-def stage_a_index(halo):
-    index = np.full((8, 16), 9, np.int64)
-    for pi in range(2):
-        for a in range(2):
+def placement(size, copies):
+    row = lax.broadcasted_iota(jnp.int32, (size, copies * LANES), 0)
+    lane = lax.broadcasted_iota(jnp.int32, (size, copies * LANES), 1)
+    hit = lane == row
+    for i in range(1, copies):
+        hit = jnp.logical_or(hit, lane == row + i * (LANES + size))
+    return hit.astype(F32).astype(BF16)
+
+
+def expand_stage_a(w, own_ref, halo_ref):
+    spread = jnp.dot(w, placement(32, 4), preferred_element_type=F32)
+    own_ref[...] = jnp.zeros_like(own_ref)
+    halo_ref[...] = jnp.zeros_like(halo_ref)
+    for ref, halo in ((own_ref, False), (halo_ref, True)):
+        for pi in range(2):
             for ri in range(2):
                 for shift in range(2):
+                    total = jnp.zeros((32, LANES), F32)
                     for ro in range(2):
                         for po in range(2):
-                            if halo:
-                                if ri != ro:
-                                    continue
-                                ky = 0 if ri == 0 else 2
-                            else:
-                                ky = ri - ro + 1
-                            if shift == 0:
-                                kx = pi - po + 1
-                            elif pi != po:
-                                kx = 0 if pi == 1 else 2
-                            else:
+                            if halo and ri != ro:
                                 continue
-                            index[(pi * 2 + a) * 2 + ri, ((shift * 2 + a) * 2 + ro) * 2 + po] = ky * 3 + kx
-    return index
-
-
-def down_own_index():
-    index = np.full((4, 2), 9, np.int64)
-    for row in range(2):
-        for par in range(2):
-            index[row * 2 + par, 0] = row * 3 + par
-        index[row * 2, 1] = row * 3 + 2
-    return index
-
-
-def down_halo_index():
-    index = np.full((4, 4), 9, np.int64)
-    for a in range(2):
-        for par in range(2):
-            index[a * 2 + par, a * 2] = 6 + par
-        index[a * 2, a * 2 + 1] = 8
-    return index
-
-
-def mid_index():
-    index = np.full((6, 6), 9, np.int64)
-    for src, ky in enumerate((1, 0, 2)):
-        for kx in range(3):
+                            if shift and pi == po:
+                                continue
+                            ky = 2 * ri if halo else ri - ro + 1
+                            kx = (0 if pi == 1 else 2) if shift else pi - po + 1
+                            tap, i = ky * 3 + kx, ro * 2 + po
+                            total += spread[tap * 32:(tap + 1) * 32, i * LANES:(i + 1) * LANES]
+                    block = total.astype(BF16)
+                    for a in range(2):
+                        row, col = ((pi * 2 + a) * 2 + ri) * 32, (shift * 2 + a) * LANES
+                        ref[row:row + 32, col:col + LANES] = block
+
+
+def expand_down(w_ref, own_ref, halo_ref):
+    own_ref[...] = jnp.zeros_like(own_ref)
+    halo_ref[...] = jnp.zeros_like(halo_ref)
+    for par in range(2):
+        for shift in range(2 - par):
+            kx = 2 if shift else par
+            for row in range(2):
+                at = (row * 2 + par) * 32
+                own_ref[at:at + 32, shift * LANES:(shift + 1) * LANES] = w_ref[row * 3 + kx]
             for a in range(2):
-                index[src * 2 + a, kx * 2 + a] = ky * 3 + kx
-    return index
+                at, col = (a * 2 + par) * 32, (a * 2 + shift) * LANES
+                halo_ref[at:at + 32, col:col + LANES] = w_ref[6 + kx]
+
+
+def expand_blocks(w_in_ref, w_mid_ref, w_out_ref, win_ref, wmid_ref, wout_ref):
+    spot = placement(64, 2)
+    for j in range(win_ref.shape[0]):
+        w_in = w_in_ref[j].astype(F32).T.astype(BF16)
+        spread = jnp.dot(w_in, spot, preferred_element_type=F32).astype(BF16)
+        for a in range(2):
+            win_ref[j, a * LANES:(a + 1) * LANES, :] = spread[:, a * LANES:(a + 1) * LANES]
+        for src, ky in enumerate((1, 0, 2)):
+            for kx in range(3):
+                spread = jnp.dot(w_mid_ref[j, ky * 3 + kx], spot, preferred_element_type=F32).astype(BF16)
+                for a in range(2):
+                    at = (src * 2 + a) * 64
+                    wmid_ref[j, at:at + 64, kx * LANES:(kx + 1) * LANES] = spread[:, a * LANES:(a + 1) * LANES]
+        zeros = jnp.zeros((64, LANES), BF16)
+        for a in range(2):
+            for b in range(2):
+                wout_ref[j, a * 64:(a + 1) * 64, b * LANES:(b + 1) * LANES] = w_out_ref[j] if a == b else zeros
 
 
 def kernel(
-    n, img_hbm, wao_ref, wah_ref, wdo_ref, wdh_ref, win_ref, wmid_ref, wout_ref, bn_ref, out_hbm,
+    n, img_hbm, wa_hbm, wd_hbm, wi_hbm, wm_hbm, wo_hbm, ba_hbm, bd_hbm, bi_hbm, bm_hbm, bo_hbm, out_hbm,
+    wa_raw, wd_raw, wi_raw, wm_raw, wo_raw, ba_raw, bd_raw, bi_raw, bm_raw, bo_raw, w_sem,
+    wao_ref, wah_ref, wdo_ref, wdh_ref, win_ref, wmid_ref, wout_ref, bn_ref,
     ximg, xabove, xbelow, tscr, za, rsend, rrecv, zd, h, zi, u2, habove, hbelow, zm, zo, stats, recv,
     img_sem, isend_sem, irecv_sem, rsend_sem, rrecv_sem, hsend_sem, hrecv_sem, ssem, rsem, out_sem,
 ):
@@ -98,7 +103,17 @@
         pltpu.make_async_copy(img_hbm.at[:, pl.ds(c * per, per)], ximg.at[:, pl.ds(c * per, per)], img_sem.at[c])
         for c in range(chunks)
     ]
+    params = [
+        pltpu.make_async_copy(src, dst, w_sem.at[i])
+        for i, (src, dst) in enumerate((
+            (wa_hbm, wa_raw), (wd_hbm, wd_raw), (wi_hbm, wi_raw), (wm_hbm, wm_raw), (wo_hbm, wo_raw),
+            (ba_hbm, ba_raw), (bd_hbm, bd_raw), (bi_hbm, bi_raw), (bm_hbm, bm_raw), (bo_hbm, bo_raw),
+        ))
+    ]
+    params[0].start()
     for copy in local_img:
+        copy.start()
+    for copy in params[1:]:
         copy.start()
 
     xabove[...] = jnp.zeros_like(xabove)
@@ -143,6 +158,9 @@
         @pl.when(has_prev)
         def _():
             img_up(c).start()
+
+    params[0].wait()
+    expand_stage_a(wa_raw[...], wao_ref, wah_ref)
 
     def shift_down(y):
         row = lax.broadcasted_iota(jnp.int32, y.shape, 0)
@@ -173,7 +191,8 @@
             to_dev(stats.at[k], recv.at[k, d - 1], ssem.at[k], rsem.at[k], lax.rem(me + d, n)).start()
             return carry
 
-        lax.fori_loop(1, n, send, 0)
+        for d in sorted(range(1, n), key=lambda d: abs(2 * d - n)):
+            send(d, 0)
         to_dev(recv.at[k], recv.at[k], ssem.at[k], rsem.at[k], me).wait_recv()
         return mine + jnp.sum(recv[k], axis=0)
 
@@ -213,6 +232,17 @@
             return carry
 
         lax.fori_loop(c * per, (c + 1) * per, own_a, 0)
+
+    for copy in params[1:]:
+        copy.wait()
+    expand_down(wd_raw, wdo_ref, wdh_ref)
+    expand_blocks(wi_raw, wm_raw, wo_raw, win_ref, wmid_ref, wout_ref)
+    bn_ref[0] = jnp.concatenate([ba_raw[0]] * 4, axis=1)
+    bn_ref[1] = bd_raw[...]
+    for j in range(wi_raw.shape[0]):
+        bn_ref[2 + 3 * j] = jnp.concatenate([bi_raw[j]] * 2, axis=1)
+        bn_ref[3 + 3 * j] = jnp.concatenate([bm_raw[j]] * 2, axis=1)
+        bn_ref[4 + 3 * j] = bo_raw[j]
 
     acc = zero_acc
     for c in range(chunks):
@@ -396,31 +426,30 @@
         blocks = w_in.shape[0]
         chunks = min(8, pairs)
         img = jnp.transpose(images, (0, 1, 3, 2)).reshape(2, pairs, rows, chan_a, width)
-        taps_a = w_a[0].reshape(9, chan_a, chan_a)
-        wao = place_taps(taps_a, stage_a_index(False))
-        wah = place_taps(taps_a, stage_a_index(True))
-        taps_d = w_down.reshape(9, chan_a, LANES)
-        wdo = place_taps(taps_d, down_own_index())
-        wdh = place_taps(taps_d, down_halo_index())
-        eye = np.array([[0, 1], [1, 0]], np.int64)
-        win = jnp.stack([place_taps(w_in[j][None], eye) for j in range(blocks)])
-        wmid = jnp.stack([place_taps(w_mid[j].reshape(9, 64, 64), mid_index()) for j in range(blocks)])
-        wout = jnp.stack([place_taps(w_out[j][None], eye) for j in range(blocks)])
-        layers = [jnp.tile(bn_a[0], (1, 4)), bn_down]
-        for j in range(blocks):
-            layers += [jnp.tile(bn_in[j], (1, 2)), jnp.tile(bn_mid[j], (1, 2)), bn_out[j]]
-        bn_all = jnp.stack(layers)
-        steps = len(layers)
-
-        vmem = pl.BlockSpec(memory_space=pltpu.VMEM)
+        taps = w_a.shape[1] * w_a.shape[2]
+        raw = [
+            w_a.reshape(taps * chan_a, chan_a), w_down.reshape(taps, chan_a, LANES), jnp.transpose(w_in, (0, 2, 1)),
+            w_mid.reshape(blocks, taps, 64, 64), w_out, bn_a, bn_down, bn_in, bn_mid, bn_out,
+        ]
+        steps = 2 + 3 * blocks
+
         anyspace = pl.BlockSpec(memory_space=pl.ANY)
         dma = pltpu.SemaphoreType.DMA
         out = pl.pallas_call(
             functools.partial(kernel, n),
             out_shape=jax.ShapeDtypeStruct((2, pairs, half_w, LANES), BF16),
-            in_specs=[anyspace] + [vmem] * 8,
+            in_specs=[pl.BlockSpec(memory_space=pltpu.HBM)] * 11,
             out_specs=anyspace,
-            scratch_shapes=[
+            scratch_shapes=[pltpu.VMEM(x.shape, x.dtype) for x in raw] + [
+                dma((len(raw),)),
+                pltpu.VMEM((2 * LANES, 4 * LANES), BF16),
+                pltpu.VMEM((2 * LANES, 4 * LANES), BF16),
+                pltpu.VMEM((LANES, 2 * LANES), BF16),
+                pltpu.VMEM((LANES, 4 * LANES), BF16),
+                pltpu.VMEM((blocks, 2 * LANES, LANES), BF16),
+                pltpu.VMEM((blocks, 3 * LANES, 3 * LANES), BF16),
+                pltpu.VMEM((blocks, LANES, 2 * LANES), BF16),
+                pltpu.VMEM((steps, 2, LANES), F32),
                 pltpu.VMEM((2, pairs, rows, chan_a, width), BF16),
                 pltpu.VMEM((2, pairs, chan_a, width), BF16),
                 pltpu.VMEM((2, pairs, chan_a, width), BF16),
@@ -452,7 +481,7 @@
             compiler_params=pltpu.CompilerParams(
                 collective_id=0, has_side_effects=True, vmem_limit_bytes=60 * 1024 * 1024
             ),
-        )(img, wao, wah, wdo, wdh, win, wmid, wout, bn_all)
+        )(img, *raw)
         return out.reshape(count, rows // 2, half_w, LANES)
 
     act_spec = P("dp", "sp", None, None)

time: 185 us -> 162 us (0.88)
  local copies, waits for them, and re-layouts: 15.6 us -> 3.14 us
  other arithmetic: 4.29 us -> 0 us
  Pallas kernels: 162 us -> 158 us
  matrix products: 3 us -> 0 us
    another operation x29 -> x0, local copies, waits for them, and re-layouts: 5.51 us -> none  [the longest x3 1.43 us: forward(): jnp.stack([place_taps(w_mid[j].reshape(9, 64, 64), mid_index()) for j in...]
    unnamed x33 -> x1, local copies, waits for them, and re-layouts: 6.6 us -> 3.14 us
    reshape x2 -> x0, local copies, waits for them, and re-layouts: 3.44 us -> none  [place_taps(): return blocks.astype(BF16).reshape(rows * ci, cols * co)]
    pallas_call x1, Pallas kernels: 162 us -> 158 us  [forward(): pl.pallas_call(functools.partial(kernel, n), out_shape=jax.ShapeDtypeStru...]
    another operation x5 -> x0, other arithmetic: 3.21 us -> none  [the longest x1 1.03 us: forward(): jnp.stack([place_taps(w_mid[j].reshape(9, 64, 64), mid_index()) for j in...]
    dot_general x7 -> x0, matrix products: 3 us -> none  [place_taps(): jnp.einsum('rct,tio->rico', jnp.asarray(pick, BF16), taps, preferred_elem...]
where the time goes in v2:
time: 162 us; the launch traced here: 161 us
  Pallas kernels  158 us (98%)
  local copies, waits for them, and re-layouts  3.14 us (2%)
    pallas_call x1, Pallas kernels, forward(): pl.pallas_call(functools.partial(kernel, n), out_shape=jax.ShapeDtypeStru...  158 us

profile of v2, /device:TPU:97, one launch (start us, length us, event | category | flops | bytes accessed | tf_op | source)
XLA Modules:
  0.0 161.5 jit_solution(870134917805876629)
XLA Ops:
  0.0 158.3 %shard_map.109 = bf16[2,16,256,128]{3,2,1,0:T(8,128)(2,1)} custom-call(bf16[2,16,2,32,512]{4,3,2,1,0:T(8,128)(2,1)} %bitcast.11, bf16[288,32]{1,0:T(8,128)(2,1)} %bitcast.13, bf16[9,32,128]{2,1,0:T(8,128)(2,1)} %bitcast.14, bf16[3,64,128]{2,1,0:T(8,128)(2,1)} %bitcast.15, bf16[3,9,64,64]{3,2,1,0:T(8,128)(2,1)} %bitcast.12, bf16[3,64,128]{2,1,0:T(8,128)(2,1)} %wo_hbm.1, ...), custom_call_target="tpu_custom_call" | custom-call | tf_op jit(solution)/shard_map/pallas_call | solution.py:438
  158.4 3.1 %copy.14 = bf16[32,1,256,128]{3,2,1,0:T(8,128)(2,1)} copy(bf16[32,1,256,128]{3,2,1,0:T(8,128)(2,1)} %bitcast.10) | data formatting | bytes 4194304

commit v3 on v2

--- a/solution.py
+++ b/solution.py
@@ -10,8 +10,42 @@
 NORM_EPS = 1e-5
 MESH = pl.DeviceIdType.MESH
 LANES = 128
+IMG_CUTS = (5, 5, 4, 2)
+LATE_CUTS = (4, 4, 2, 1)
+EARLY_CUTS = (1, 4)
+OUT_CUTS = (6, 6, 3, 1)
+ROW_EARLY, MID_EARLY, OF_PAIRS = 3, 5, 16
 F32 = jnp.float32
 BF16 = jnp.bfloat16
+
+
+def cuts(first, last, weights):
+    total, seen, edge, spans = sum(weights), 0, first, []
+    for weight in weights:
+        seen += weight
+        end = first + (last - first) * seen // total
+        if end > edge:
+            spans.append((edge, end - edge))
+        edge = end
+    return spans
+
+
+def over(span, body, carry=0, step=1):
+    start, length = span
+    trips = length // step
+
+    def trip(i, carry):
+        for k in range(step):
+            carry = body(start + i * step + k, carry)
+        return carry
+
+    if trips == 1:
+        carry = trip(0, carry)
+    elif trips > 1:
+        carry = lax.fori_loop(0, trips, trip, carry)
+    for q in range(start + trips * step, start + length):
+        carry = body(q, carry)
+    return carry
 
 
 def placement(size, copies):
@@ -85,24 +119,29 @@
     n, img_hbm, wa_hbm, wd_hbm, wi_hbm, wm_hbm, wo_hbm, ba_hbm, bd_hbm, bi_hbm, bm_hbm, bo_hbm, out_hbm,
     wa_raw, wd_raw, wi_raw, wm_raw, wo_raw, ba_raw, bd_raw, bi_raw, bm_raw, bo_raw, w_sem,
     wao_ref, wah_ref, wdo_ref, wdh_ref, win_ref, wmid_ref, wout_ref, bn_ref,
-    ximg, xabove, xbelow, tscr, za, rsend, rrecv, zd, h, zi, u2, habove, hbelow, zm, zo, stats, recv,
-    img_sem, isend_sem, irecv_sem, rsend_sem, rrecv_sem, hsend_sem, hrecv_sem, ssem, rsem, out_sem,
+    ximg, xabove, xbelow, tscr, za, rsend, rrecv, zrow, zrow_in, zd, h, zi, u2, habove, hbelow, zabove, zbelow,
+    zm, zo, stats, recv,
+    img_sem, isend_sem, irecv_sem, rsend_sem, rrecv_sem, zsend_sem, zrecv_sem, hsend_sem, hrecv_sem,
+    esend_sem, erecv_sem, ssem, rsem, out_sem,
 ):
     me = lax.axis_index("sp")
     nxt, prv = me + 1, me - 1
     has_next, has_prev = me < n - 1, me > 0
-    pairs, chunks = ximg.shape[1], isend_sem.shape[1]
-    per = pairs // chunks
+    pairs = ximg.shape[1]
     half_w = tscr.shape[0] // 2
     full_w = tscr.shape[0]
-    rows_all = lax.axis_size("sp")
-    count_a = float(2 * pairs * 2 * full_w) * rows_all
-    count_b = float(2 * pairs * half_w) * rows_all
-
-    local_img = [
-        pltpu.make_async_copy(img_hbm.at[:, pl.ds(c * per, per)], ximg.at[:, pl.ds(c * per, per)], img_sem.at[c])
-        for c in range(chunks)
-    ]
+    count_a = float(2 * pairs * 2 * full_w * n)
+    count_b = float(2 * pairs * half_w * n)
+    everything = (0, pairs)
+
+    img_load = cuts(0, pairs, (4, 4, 4, 4))
+    img_spans = cuts(0, pairs, IMG_CUTS)
+    row_early, mid_early = zrow.shape[0], zabove.shape[1]
+    row_spans = cuts(row_early, pairs, LATE_CUTS)
+    mid_spans = cuts(mid_early, pairs, LATE_CUTS)
+    early_spans = cuts(0, mid_early, EARLY_CUTS)
+    out_spans = cuts(0, pairs, OUT_CUTS)
+
     params = [
         pltpu.make_async_copy(src, dst, w_sem.at[i])
         for i, (src, dst) in enumerate((
@@ -110,31 +149,30 @@
             (ba_hbm, ba_raw), (bd_hbm, bd_raw), (bi_hbm, bi_raw), (bm_hbm, bm_raw), (bo_hbm, bo_raw),
         ))
     ]
+    local_img = [
+        pltpu.make_async_copy(img_hbm.at[:, pl.ds(*span)], ximg.at[:, pl.ds(*span)], img_sem.at[c])
+        for c, span in enumerate(img_load)
+    ]
+    barrier = pltpu.get_barrier_semaphore()
+    for d in range(1, n):
+        pl.semaphore_signal(barrier, inc=1, device_id={"sp": lax.rem(me + d, n)}, device_id_type=MESH)
     params[0].start()
     for copy in local_img:
         copy.start()
     for copy in params[1:]:
         copy.start()
 
-    xabove[...] = jnp.zeros_like(xabove)
-    xbelow[...] = jnp.zeros_like(xbelow)
-
     @pl.when(me == n - 1)
     def _():
+        xbelow[...] = jnp.zeros_like(xbelow)
         rrecv[...] = jnp.zeros_like(rrecv)
         hbelow[...] = jnp.zeros_like(hbelow)
 
     @pl.when(me == 0)
     def _():
+        xabove[...] = jnp.zeros_like(xabove)
         habove[...] = jnp.zeros_like(habove)
 
-    barrier = pltpu.get_barrier_semaphore()
-
-    def greet(d, carry):
-        pl.semaphore_signal(barrier, inc=1, device_id={"sp": lax.rem(me + d, n)}, device_id_type=MESH)
-        return carry
-
-    lax.fori_loop(1, n, greet, 0)
     pl.semaphore_wait(barrier, n - 1)
 
     def to_dev(src, dst, send_sem, recv_sem, dev):
@@ -143,21 +181,33 @@
         )
 
     def img_down(c):
-        part = pl.ds(c * per, per)
+        part = pl.ds(*img_spans[c])
         return to_dev(img_hbm.at[:, part, 1], xabove.at[:, part], isend_sem.at[0, c], irecv_sem.at[0, c], nxt)
 
     def img_up(c):
-        part = pl.ds(c * per, per)
+        part = pl.ds(*img_spans[c])
         return to_dev(img_hbm.at[:, part, 0], xbelow.at[:, part], isend_sem.at[1, c], irecv_sem.at[1, c], prv)
 
-    for c in range(chunks):
+    def exchange(down, up, c):
         @pl.when(has_next)
         def _():
-            img_down(c).start()
+            down(c).start()
 
         @pl.when(has_prev)
         def _():
-            img_up(c).start()
+            up(c).start()
+
+    def arrived(down, up, c):
+        @pl.when(has_prev)
+        def _():
+            down(c).wait_recv()
+
+        @pl.when(has_next)
+        def _():
+            up(c).wait_recv()
+
+    for c in range(len(img_spans)):
+        exchange(img_down, img_up, c)
 
     params[0].wait()
     expand_stage_a(wa_raw[...], wao_ref, wah_ref)
@@ -176,7 +226,7 @@
 
     zero_acc = (jnp.zeros((8, LANES), F32), jnp.zeros((8, LANES), F32))
 
-    def group_stats(k, acc, group):
+    def group_stats(k, acc, group, meanwhile=None):
         def fold(v):
             width = group
             while width < LANES:
@@ -186,13 +236,10 @@
 
         mine = jnp.concatenate([fold(acc[0]), fold(acc[1])], axis=0)
         stats[k] = mine
-
-        def send(d, carry):
+        for d in sorted(range(1, n), key=lambda d: abs(2 * d - n)):
             to_dev(stats.at[k], recv.at[k, d - 1], ssem.at[k], rsem.at[k], lax.rem(me + d, n)).start()
-            return carry
-
-        for d in sorted(range(1, n), key=lambda d: abs(2 * d - n)):
-            send(d, 0)
+        if meanwhile is not None:
+            meanwhile()
         to_dev(recv.at[k], recv.at[k], ssem.at[k], rsem.at[k], me).wait_recv()
         return mine + jnp.sum(recv[k], axis=0)
 
@@ -219,19 +266,16 @@
         cross = y[:, 2 * LANES:]
         return y[:, : 2 * LANES] + jnp.where(even_lane, shift_down(cross), shift_up(cross))
 
-    for c in range(chunks):
+    def own_a(q, carry):
+        x = jnp.concatenate([ximg[0, q].reshape(2 * 32, full_w), ximg[1, q].reshape(2 * 32, full_w)], axis=0)
+        z = stage_a_part(x, wao_ref)
+        za[0, q] = z[:, :LANES]
+        za[1, q] = z[:, LANES:]
+        return carry
+
+    for c, span in enumerate(img_load):
         local_img[c].wait()
-
-        def own_a(q, carry):
-            x = jnp.concatenate(
-                [ximg[0, q].reshape(2 * 32, full_w), ximg[1, q].reshape(2 * 32, full_w)], axis=0
-            )
-            z = stage_a_part(x, wao_ref)
-            za[0, q] = z[:, :LANES]
-            za[1, q] = z[:, LANES:]
-            return carry
-
-        lax.fori_loop(c * per, (c + 1) * per, own_a, 0)
+        over(span, own_a)
 
     for copy in params[1:]:
         copy.wait()
@@ -244,78 +288,120 @@
         bn_ref[3 + 3 * j] = jnp.concatenate([bm_raw[j]] * 2, axis=1)
         bn_ref[4 + 3 * j] = bo_raw[j]
 
+    def halo_a(q, acc):
+        x = jnp.concatenate([xabove[0, q], xbelow[0, q], xabove[1, q], xbelow[1, q]], axis=0)
+        z = stage_a_part(x, wah_ref)
+        z0 = za[0, q] + z[:, :LANES]
+        z1 = za[1, q] + z[:, LANES:]
+        za[0, q] = z0
+        za[1, q] = z1
+        return add_stats(add_stats(acc, z0), z1)
+
     acc = zero_acc
-    for c in range(chunks):
-        @pl.when(has_prev)
-        def _():
-            img_down(c).wait_recv()
-
-        @pl.when(has_next)
-        def _():
-            img_up(c).wait_recv()
-
-        def halo_a(q, acc):
-            x = jnp.concatenate([xabove[0, q], xbelow[0, q], xabove[1, q], xbelow[1, q]], axis=0)
-            z = stage_a_part(x, wah_ref)
-            z0 = za[0, q] + z[:, :LANES]
-            z1 = za[1, q] + z[:, LANES:]
-            za[0, q] = z0
-            za[1, q] = z1
-            return add_stats(add_stats(acc, z0), z1)
-
-        acc = lax.fori_loop(c * per, (c + 1) * per, halo_a, acc)
-    norm = norm_of(0, group_stats(0, acc, 32), count_a)
+    for c, span in enumerate(img_spans):
+        arrived(img_down, img_up, c)
+        acc = over(span, halo_a, acc)
 
     lane1 = lax.broadcasted_iota(jnp.int32, (half_w, LANES), 1)
     low_lane = lane1 < 64
 
     def row_up(c):
-        part = pl.ds(c * per, per)
+        part = pl.ds(*row_spans[c])
         return to_dev(rsend.at[part], rrecv.at[part], rsend_sem.at[c], rrecv_sem.at[c], prv)
 
-    for c in range(chunks):
-        def own_down(q, carry):
-            t0 = jnp.maximum(bn(za[0, q], norm), 0.0)
-            t1 = jnp.maximum(bn(za[1, q], norm), 0.0)
-            rsend[q] = jnp.where(low_lane, t0, pltpu.roll(t1, 64, 1)).astype(BF16)
-            for a, t in enumerate((t0, t1)):
-                y = jnp.dot(t.astype(BF16), wdo_ref[...], preferred_element_type=F32)
-                zd[a, q] = y[:, :LANES] + shift_up(y[:, LANES:])
+    def early_row_up():
+        return to_dev(zrow, zrow_in, zsend_sem, zrecv_sem, prv)
+
+    def first_rows(t0, t1):
+        return jnp.where(low_lane, t0, pltpu.roll(t1, 64, 1))
+
+    def send_early_rows():
+        def pack(q, carry):
+            zrow[q] = first_rows(za[0, q], za[1, q])
             return carry
 
-        lax.fori_loop(c * per, (c + 1) * per, own_down, 0)
+        over((0, row_early), pack)
 
         @pl.when(has_prev)
         def _():
+            early_row_up().start()
+
+    norm = norm_of(0, group_stats(0, acc, 32, send_early_rows if row_early else None), count_a)
+
+    def pack_row(q, carry):
+        rsend[q] = jnp.maximum(bn(first_rows(za[0, q], za[1, q]), norm), 0.0).astype(BF16)
+        return carry
+
+    for c, span in enumerate(row_spans):
+        over(span, pack_row)
+
+        @pl.when(has_prev)
+        def _():
             row_up(c).start()
 
-    acc = zero_acc
-    for c in range(chunks):
+    def own_down(q, carry):
+        for a in range(2):
+            t = jnp.maximum(bn(za[a, q], norm), 0.0).astype(BF16)
+            y = jnp.dot(t, wdo_ref[...], preferred_element_type=F32)
+            zd[a, q] = y[:, :LANES] + shift_up(y[:, LANES:])
+        return carry
+
+    over(everything, own_down)
+
+    if row_early:
         @pl.when(has_next)
         def _():
+            early_row_up().wait_recv()
+
+            def norm_row(q, carry):
+                rrecv[q] = jnp.maximum(bn(zrow_in[q], norm), 0.0).astype(BF16)
+                return carry
+
+            over((0, row_early), norm_row)
+
+    def halo_down(q, acc):
+        y = jnp.dot(rrecv[q], wdh_ref[...], preferred_element_type=F32)
+        for a in range(2):
+            lo = 2 * a * LANES
+            z = zd[a, q] + y[:, lo:lo + LANES] + shift_up(y[:, lo + LANES:lo + 2 * LANES])
+            zd[a, q] = z
+            acc = add_stats(acc, z)
+        return acc
+
+    acc = over((0, row_early), halo_down, zero_acc)
+    for c, span in enumerate(row_spans):
+        @pl.when(has_next)
+        def _():
             row_up(c).wait_recv()
 
-        def halo_down(q, acc):
-            y = jnp.dot(rrecv[q], wdh_ref[...], preferred_element_type=F32)
-            for a in range(2):
-                lo = 2 * a * LANES
-                z = zd[a, q] + y[:, lo:lo + LANES] + shift_up(y[:, lo + LANES:lo + 2 * LANES])
-                zd[a, q] = z
-                acc = add_stats(acc, z)
-            return acc
-
-        acc = lax.fori_loop(c * per, (c + 1) * per, halo_down, acc)
+        acc = over(span, halo_down, acc)
     norm = norm_of(1, group_stats(1, acc, LANES), count_b)
 
     blocks = win_ref.shape[0]
 
-    def mid_down(j, c):
-        part = pl.ds(c * per, per)
-        return to_dev(u2.at[j, part], habove.at[j, part], hsend_sem.at[j, 0, c], hrecv_sem.at[j, 0, c], nxt)
-
-    def mid_up(j, c):
-        part = pl.ds(c * per, per)
-        return to_dev(u2.at[j, part], hbelow.at[j, part], hsend_sem.at[j, 1, c], hrecv_sem.at[j, 1, c], prv)
+    def mid_down(j):
+        def copy(c):
+            part = pl.ds(*mid_spans[c])
+            return to_dev(u2.at[j, part], habove.at[j, part], hsend_sem.at[j, 0, c], hrecv_sem.at[j, 0, c], nxt)
+        return copy
+
+    def mid_up(j):
+        def copy(c):
+            part = pl.ds(*mid_spans[c])
+            return to_dev(u2.at[j, part], hbelow.at[j, part], hsend_sem.at[j, 1, c], hrecv_sem.at[j, 1, c], prv)
+        return copy
+
+    def early_down(j):
+        def copy(c):
+            part = pl.ds(*early_spans[c])
+            return to_dev(zi.at[j, part], zabove.at[j, part], esend_sem.at[j, 0, c], erecv_sem.at[j, 0, c], nxt)
+        return copy
+
+    def early_up(j):
+        def copy(c):
+            part = pl.ds(*early_spans[c])
+            return to_dev(zi.at[j, part], zbelow.at[j, part], esend_sem.at[j, 1, c], erecv_sem.at[j, 1, c], prv)
+        return copy
 
     for j in range(blocks):
         def layer_in(q, acc):
@@ -329,45 +415,62 @@
                 h[a, q] = t
                 parts.append(t)
             z = jnp.dot(jnp.concatenate(parts, axis=1), win_ref[j], preferred_element_type=F32)
-            zi[q] = z
+            zi[j, q] = z
             return add_stats(acc, z)
 
-        acc = lax.fori_loop(0, pairs, layer_in, zero_acc)
-        norm = norm_of(2 + 3 * j, group_stats(2 + 3 * j, acc, 64), count_b)
-
-        for c in range(chunks):
-            def act_in(q, carry):
-                u2[j, q] = jnp.maximum(bn(zi[q], norm), 0.0).astype(BF16)
+        acc, done = zero_acc, 0
+        if early_spans:
+            done = early_spans[0][1]
+            acc = over(early_spans[0], layer_in, acc)
+            exchange(early_down(j), early_up(j), 0)
+        acc = over((done, pairs - done), layer_in, acc, 2)
+
+        def send_early():
+            for c in range(1, len(early_spans)):
+                exchange(early_down(j), early_up(j), c)
+
+        norm = norm_of(2 + 3 * j, group_stats(2 + 3 * j, acc, 64, send_early), count_b)
+
+        def act_in(q, carry):
+            u2[j, q] = jnp.maximum(bn(zi[j, q], norm), 0.0).astype(BF16)
+            return carry
+
+        for c, span in enumerate(mid_spans):
+            over(span, act_in)
+            exchange(mid_down(j), mid_up(j), c)
+        over((0, mid_early), act_in)
+
+        if early_spans:
+            for c in range(len(early_spans)):
+                arrived(early_down(j), early_up(j), c)
+
+            def act_above(q, carry):
+                habove[j, q] = jnp.maximum(bn(zabove[j, q], norm), 0.0).astype(BF16)
                 return carry
 
-            lax.fori_loop(c * per, (c + 1) * per, act_in, 0)
+            def act_below(q, carry):
+                hbelow[j, q] = jnp.maximum(bn(zbelow[j, q], norm), 0.0).astype(BF16)
+                return carry
+
+            @pl.when(has_prev)
+            def _():
+                over((0, mid_early), act_above)
 
             @pl.when(has_next)
             def _():
-                mid_down(j, c).start()
-
-            @pl.when(has_prev)
-            def _():
-                mid_up(j, c).start()
-
-        acc = zero_acc
-        for c in range(chunks):
-            @pl.when(has_prev)
-            def _():
-                mid_down(j, c).wait_recv()
-
-            @pl.when(has_next)
-            def _():
-                mid_up(j, c).wait_recv()
-
-            def layer_mid(q, acc):
-                lhs = jnp.concatenate([u2[j, q], habove[j, q], hbelow[j, q]], axis=1)
-                y = jnp.dot(lhs, wmid_ref[j], preferred_element_type=F32)
-                z = shift_down(y[:, :LANES]) + y[:, LANES:2 * LANES] + shift_up(y[:, 2 * LANES:])
-                zm[q] = z
-                return add_stats(acc, z)
-
-            acc = lax.fori_loop(c * per, (c + 1) * per, layer_mid, acc)
+                over((0, mid_early), act_below)
+
+        def layer_mid(q, acc):
+            lhs = jnp.concatenate([u2[j, q], habove[j, q], hbelow[j, q]], axis=1)
+            y = jnp.dot(lhs, wmid_ref[j], preferred_element_type=F32)
+            z = shift_down(y[:, :LANES]) + y[:, LANES:2 * LANES] + shift_up(y[:, 2 * LANES:])
+            zm[q] = z
+            return add_stats(acc, z)
+
+        acc = over((0, mid_early), layer_mid, zero_acc)
+        for c, span in enumerate(mid_spans):
+            arrived(mid_down(j), mid_up(j), c)
+            acc = over(span, layer_mid, acc)
         norm = norm_of(3 + 3 * j, group_stats(3 + 3 * j, acc, 64), count_b)
 
         def layer_out(q, acc):
@@ -379,20 +482,20 @@
                 acc = add_stats(acc, z)
             return acc
 
-        acc = lax.fori_loop(0, pairs, layer_out, zero_acc)
+        acc = over(everything, layer_out, zero_acc, 2)
         norm = norm_of(4 + 3 * j, group_stats(4 + 3 * j, acc, LANES), count_b)
 
     def store(c):
-        part = pl.ds(c * per, per)
+        part = pl.ds(*out_spans[c])
         return pltpu.make_async_copy(h.at[:, part], out_hbm.at[:, part], out_sem.at[c])
 
-    for c in range(chunks):
-        def final(q, carry):
-            for a in range(2):
-                h[a, q] = jnp.maximum(bn(zo[a, q], norm) + h[a, q].astype(F32), 0.0).astype(BF16)
-            return carry
-
-        lax.fori_loop(c * per, (c + 1) * per, final, 0)
+    def final(q, carry):
+        for a in range(2):
+            h[a, q] = jnp.maximum(bn(zo[a, q], norm) + h[a, q].astype(F32), 0.0).astype(BF16)
+        return carry
+
+    for c, span in enumerate(out_spans):
+        over(span, final)
         store(c).start()
 
     for k in range(stats.shape[0]):
@@ -400,20 +503,29 @@
 
     @pl.when(has_next)
     def _():
-        for c in range(chunks):
+        for c in range(len(img_spans)):
             img_down(c).wait_send()
-            for j in range(blocks):
-                mid_down(j, c).wait_send()
+        for j in range(blocks):
+            for c in range(len(mid_spans)):
+                mid_down(j)(c).wait_send()
+            for c in range(len(early_spans)):
+                early_down(j)(c).wait_send()
 
     @pl.when(has_prev)
     def _():
-        for c in range(chunks):
+        for c in range(len(img_spans)):
             img_up(c).wait_send()
+        for c in range(len(row_spans)):
             row_up(c).wait_send()
-            for j in range(blocks):
-                mid_up(j, c).wait_send()
-
-    for c in range(chunks):
+        if row_early:
+            early_row_up().wait_send()
+        for j in range(blocks):
+            for c in range(len(mid_spans)):
+                mid_up(j)(c).wait_send()
+            for c in range(len(early_spans)):
+                early_up(j)(c).wait_send()
+
+    for c in range(len(out_spans)):
         store(c).wait()
 
 
@@ -424,7 +536,7 @@
         count, rows, width, chan_a = images.shape
         pairs, half_w = count // 2, width // 2
         blocks = w_in.shape[0]
-        chunks = min(8, pairs)
+        row_early, mid_early = pairs * ROW_EARLY // OF_PAIRS, pairs * MID_EARLY // OF_PAIRS
         img = jnp.transpose(images, (0, 1, 3, 2)).reshape(2, pairs, rows, chan_a, width)
         taps = w_a.shape[1] * w_a.shape[2]
         raw = [
@@ -457,26 +569,34 @@
                 pltpu.VMEM((2, pairs, half_w, LANES), F32),
                 pltpu.VMEM((pairs, half_w, LANES), BF16),
                 pltpu.VMEM((pairs, half_w, LANES), BF16),
+                pltpu.VMEM((row_early, half_w, LANES), F32),
+                pltpu.VMEM((row_early, half_w, LANES), F32),
                 pltpu.VMEM((2, pairs, half_w, LANES), F32),
                 pltpu.VMEM((2, pairs, half_w, LANES), BF16),
-                pltpu.VMEM((pairs, half_w, LANES), F32),
+                pltpu.VMEM((blocks, pairs, half_w, LANES), F32),
                 pltpu.VMEM((blocks, pairs, half_w, LANES), BF16),
                 pltpu.VMEM((blocks, pairs, half_w, LANES), BF16),
                 pltpu.VMEM((blocks, pairs, half_w, LANES), BF16),
+                pltpu.VMEM((blocks, mid_early, half_w, LANES), F32),
+                pltpu.VMEM((blocks, mid_early, half_w, LANES), F32),
                 pltpu.VMEM((pairs, half_w, LANES), F32),
                 pltpu.VMEM((2, pairs, half_w, LANES), F32),
                 pltpu.VMEM((steps, 2, LANES), F32),
                 pltpu.VMEM((steps, n - 1, 2, LANES), F32),
-                dma((chunks,)),
-                dma((2, chunks)),
-                dma((2, chunks)),
-                dma((chunks,)),
-                dma((chunks,)),
-                dma((blocks, 2, chunks)),
-                dma((blocks, 2, chunks)),
+                dma((4,)),
+                dma((2, len(IMG_CUTS))),
+                dma((2, len(IMG_CUTS))),
+                dma((len(LATE_CUTS),)),
+                dma((len(LATE_CUTS),)),
+                dma,
+                dma,
+                dma((blocks, 2, len(LATE_CUTS))),
+                dma((blocks, 2, len(LATE_CUTS))),
+                dma((blocks, 2, len(EARLY_CUTS))),
+                dma((blocks, 2, len(EARLY_CUTS))),
                 dma((steps,)),
                 dma((steps,)),
-                dma((chunks,)),
+                dma((len(OUT_CUTS),)),
             ],
             compiler_params=pltpu.CompilerParams(
                 collective_id=0, has_side_effects=True, vmem_limit_bytes=60 * 1024 * 1024

time: 162 us -> 157 us (0.969)
  Pallas kernels: 158 us -> 154 us
    pallas_call x1, Pallas kernels: 158 us -> 154 us  [forward(): pl.pallas_call(functools.partial(kernel, n), out_shape=jax.ShapeDtypeStru...]
where the time goes in v3:
time: 157 us
  Pallas kernels  154 us (98%)
  local copies, waits for them, and re-layouts  3.14 us (2%)
    pallas_call x1, Pallas kernels, forward(): pl.pallas_call(functools.partial(kernel, n), out_shape=jax.ShapeDtypeStru...  154 us

profile of v3, /device:TPU:97, one launch (start us, length us, event | category | flops | bytes accessed | tf_op | source)
XLA Modules:
  0.0 156.9 jit_solution(8309864286323091772)
XLA Ops:
  0.0 153.8 %shard_map.109 = bf16[2,16,256,128]{3,2,1,0:T(8,128)(2,1)} custom-call(bf16[2,16,2,32,512]{4,3,2,1,0:T(8,128)(2,1)} %bitcast.11, bf16[288,32]{1,0:T(8,128)(2,1)} %bitcast.13, bf16[9,32,128]{2,1,0:T(8,128)(2,1)} %bitcast.14, bf16[3,64,128]{2,1,0:T(8,128)(2,1)} %bitcast.15, bf16[3,9,64,64]{3,2,1,0:T(8,128)(2,1)} %bitcast.12, bf16[3,64,128]{2,1,0:T(8,128)(2,1)} %wo_hbm.1, ...), custom_call_target="tpu_custom_call" | custom-call | tf_op jit(solution)/shard_map/pallas_call | solution.py:550
  153.8 3.1 %copy.14 = bf16[32,1,256,128]{3,2,1,0:T(8,128)(2,1)} copy(bf16[32,1,256,128]{3,2,1,0:T(8,128)(2,1)} %bitcast.10) | data formatting | bytes 4194304

commit v4 on v3

--- a/solution.py
+++ b/solution.py
@@ -11,10 +11,10 @@
 MESH = pl.DeviceIdType.MESH
 LANES = 128
 IMG_CUTS = (5, 5, 4, 2)
-LATE_CUTS = (4, 4, 2, 1)
+LATE_CUTS = (5, 7, 3, 1)
 EARLY_CUTS = (1, 4)
 OUT_CUTS = (6, 6, 3, 1)
-ROW_EARLY, MID_EARLY, OF_PAIRS = 3, 5, 16
+ROW_EARLY, MID_EARLY, OF_PAIRS = 0, 0, 16
 F32 = jnp.float32
 BF16 = jnp.bfloat16
 
@@ -368,7 +368,7 @@
             acc = add_stats(acc, z)
         return acc
 
-    acc = over((0, row_early), halo_down, zero_acc)
+    acc = over((0, row_early), halo_down, zero_acc) if row_early else zero_acc
     for c, span in enumerate(row_spans):
         @pl.when(has_next)
         def _():

time: 157 us -> 153 us (0.975)
  Pallas kernels: 154 us -> 150 us
    pallas_call x1, Pallas kernels: 154 us -> 150 us  [forward(): pl.pallas_call(functools.partial(kernel, n), out_shape=jax.ShapeDtypeStru...]
where the time goes in v4:
time: 153 us
  Pallas kernels  150 us (98%)
  local copies, waits for them, and re-layouts  3.14 us (2%)
    pallas_call x1, Pallas kernels, forward(): pl.pallas_call(functools.partial(kernel, n), out_shape=jax.ShapeDtypeStru...  150 us
    unnamed x1, local copies, waits for them, and re-layouts  3.14 us

profile of v4, /device:TPU:97, one launch (start us, length us, event | category | flops | bytes accessed | tf_op | source)
XLA Modules:
  0.0 152.9 jit_solution(5984903769795773245)
XLA Ops:
  0.0 149.7 %shard_map.109 = bf16[2,16,256,128]{3,2,1,0:T(8,128)(2,1)} custom-call(bf16[2,16,2,32,512]{4,3,2,1,0:T(8,128)(2,1)} %bitcast.11, bf16[288,32]{1,0:T(8,128)(2,1)} %bitcast.13, bf16[9,32,128]{2,1,0:T(8,128)(2,1)} %bitcast.14, bf16[3,64,128]{2,1,0:T(8,128)(2,1)} %bitcast.15, bf16[3,9,64,64]{3,2,1,0:T(8,128)(2,1)} %bitcast.12, bf16[3,64,128]{2,1,0:T(8,128)(2,1)} %wo_hbm.1, ...), custom_call_target="tpu_custom_call" | custom-call | tf_op jit(solution)/shard_map/pallas_call | solution.py:550
  149.7 3.1 %copy.14 = bf16[32,1,256,128]{3,2,1,0:T(8,128)(2,1)} copy(bf16[32,1,256,128]{3,2,1,0:T(8,128)(2,1)} %bitcast.10) | data formatting | bytes 4194304

commit v5 on v4

--- a/solution.py
+++ b/solution.py
@@ -12,9 +12,6 @@
 LANES = 128
 IMG_CUTS = (5, 5, 4, 2)
 LATE_CUTS = (5, 7, 3, 1)
-EARLY_CUTS = (1, 4)
-OUT_CUTS = (6, 6, 3, 1)
-ROW_EARLY, MID_EARLY, OF_PAIRS = 0, 0, 16
 F32 = jnp.float32
 BF16 = jnp.bfloat16
 
@@ -116,13 +113,13 @@
 
 
 def kernel(
-    n, img_hbm, wa_hbm, wd_hbm, wi_hbm, wm_hbm, wo_hbm, ba_hbm, bd_hbm, bi_hbm, bm_hbm, bo_hbm, out_hbm,
+    n, img_hbm, wa_hbm, wd_hbm, wi_hbm, wm_hbm, wo_hbm, ba_hbm, bd_hbm, bi_hbm, bm_hbm, bo_hbm, out_ref,
     wa_raw, wd_raw, wi_raw, wm_raw, wo_raw, ba_raw, bd_raw, bi_raw, bm_raw, bo_raw, w_sem,
     wao_ref, wah_ref, wdo_ref, wdh_ref, win_ref, wmid_ref, wout_ref, bn_ref,
-    ximg, xabove, xbelow, tscr, za, rsend, rrecv, zrow, zrow_in, zd, h, zi, u2, habove, hbelow, zabove, zbelow,
+    ximg, xabove, xbelow, tscr, za, rsend, rrecv, zd, h, zi, u2, habove, hbelow,
     zm, zo, stats, recv,
-    img_sem, isend_sem, irecv_sem, rsend_sem, rrecv_sem, zsend_sem, zrecv_sem, hsend_sem, hrecv_sem,
-    esend_sem, erecv_sem, ssem, rsem, out_sem,
+    img_sem, isend_sem, irecv_sem, rsend_sem, rrecv_sem, hsend_sem, hrecv_sem,
+    ssem, rsem,
 ):
     me = lax.axis_index("sp")
     nxt, prv = me + 1, me - 1
@@ -136,11 +133,8 @@
 
     img_load = cuts(0, pairs, (4, 4, 4, 4))
     img_spans = cuts(0, pairs, IMG_CUTS)
-    row_early, mid_early = zrow.shape[0], zabove.shape[1]
-    row_spans = cuts(row_early, pairs, LATE_CUTS)
-    mid_spans = cuts(mid_early, pairs, LATE_CUTS)
-    early_spans = cuts(0, mid_early, EARLY_CUTS)
-    out_spans = cuts(0, pairs, OUT_CUTS)
+    row_spans = cuts(0, pairs, LATE_CUTS)
+    mid_spans = cuts(0, pairs, LATE_CUTS)
 
     params = [
         pltpu.make_async_copy(src, dst, w_sem.at[i])
@@ -226,7 +220,7 @@
 
     zero_acc = (jnp.zeros((8, LANES), F32), jnp.zeros((8, LANES), F32))
 
-    def group_stats(k, acc, group, meanwhile=None):
+    def group_stats(k, acc, group):
         def fold(v):
             width = group
             while width < LANES:
@@ -238,8 +232,6 @@
         stats[k] = mine
         for d in sorted(range(1, n), key=lambda d: abs(2 * d - n)):
             to_dev(stats.at[k], recv.at[k, d - 1], ssem.at[k], rsem.at[k], lax.rem(me + d, n)).start()
-        if meanwhile is not None:
-            meanwhile()
         to_dev(recv.at[k], recv.at[k], ssem.at[k], rsem.at[k], me).wait_recv()
         return mine + jnp.sum(recv[k], axis=0)
 
@@ -309,24 +301,10 @@
         part = pl.ds(*row_spans[c])
         return to_dev(rsend.at[part], rrecv.at[part], rsend_sem.at[c], rrecv_sem.at[c], prv)
 
-    def early_row_up():
-        return to_dev(zrow, zrow_in, zsend_sem, zrecv_sem, prv)
-
     def first_rows(t0, t1):
         return jnp.where(low_lane, t0, pltpu.roll(t1, 64, 1))
 
-    def send_early_rows():
-        def pack(q, carry):
-            zrow[q] = first_rows(za[0, q], za[1, q])
-            return carry
-
-        over((0, row_early), pack)
-
-        @pl.when(has_prev)
-        def _():
-            early_row_up().start()
-
-    norm = norm_of(0, group_stats(0, acc, 32, send_early_rows if row_early else None), count_a)
+    norm = norm_of(0, group_stats(0, acc, 32), count_a)
 
     def pack_row(q, carry):
         rsend[q] = jnp.maximum(bn(first_rows(za[0, q], za[1, q]), norm), 0.0).astype(BF16)
@@ -347,17 +325,6 @@
         return carry
 
     over(everything, own_down)
-
-    if row_early:
-        @pl.when(has_next)
-        def _():
-            early_row_up().wait_recv()
-
-            def norm_row(q, carry):
-                rrecv[q] = jnp.maximum(bn(zrow_in[q], norm), 0.0).astype(BF16)
-                return carry
-
-            over((0, row_early), norm_row)
 
     def halo_down(q, acc):
         y = jnp.dot(rrecv[q], wdh_ref[...], preferred_element_type=F32)
@@ -368,7 +335,7 @@
             acc = add_stats(acc, z)
         return acc
 
-    acc = over((0, row_early), halo_down, zero_acc) if row_early else zero_acc
+    acc = zero_acc
     for c, span in enumerate(row_spans):
         @pl.when(has_next)
         def _():
@@ -389,18 +356,6 @@
         def copy(c):
             part = pl.ds(*mid_spans[c])
             return to_dev(u2.at[j, part], hbelow.at[j, part], hsend_sem.at[j, 1, c], hrecv_sem.at[j, 1, c], prv)
-        return copy
-
-    def early_down(j):
-        def copy(c):
-            part = pl.ds(*early_spans[c])
-            return to_dev(zi.at[j, part], zabove.at[j, part], esend_sem.at[j, 0, c], erecv_sem.at[j, 0, c], nxt)
-        return copy
-
-    def early_up(j):
-        def copy(c):
-            part = pl.ds(*early_spans[c])
-            return to_dev(zi.at[j, part], zbelow.at[j, part], esend_sem.at[j, 1, c], erecv_sem.at[j, 1, c], prv)
         return copy
 
     for j in range(blocks):
@@ -415,51 +370,19 @@
                 h[a, q] = t
                 parts.append(t)
             z = jnp.dot(jnp.concatenate(parts, axis=1), win_ref[j], preferred_element_type=F32)
-            zi[j, q] = z
+            zi[q] = z
             return add_stats(acc, z)
 
-        acc, done = zero_acc, 0
-        if early_spans:
-            done = early_spans[0][1]
-            acc = over(early_spans[0], layer_in, acc)
-            exchange(early_down(j), early_up(j), 0)
-        acc = over((done, pairs - done), layer_in, acc, 2)
-
-        def send_early():
-            for c in range(1, len(early_spans)):
-                exchange(early_down(j), early_up(j), c)
-
-        norm = norm_of(2 + 3 * j, group_stats(2 + 3 * j, acc, 64, send_early), count_b)
+        acc = over(everything, layer_in, zero_acc, 4)
+        norm = norm_of(2 + 3 * j, group_stats(2 + 3 * j, acc, 64), count_b)
 
         def act_in(q, carry):
-            u2[j, q] = jnp.maximum(bn(zi[j, q], norm), 0.0).astype(BF16)
+            u2[j, q] = jnp.maximum(bn(zi[q], norm), 0.0).astype(BF16)
             return carry
 
         for c, span in enumerate(mid_spans):
             over(span, act_in)
             exchange(mid_down(j), mid_up(j), c)
-        over((0, mid_early), act_in)
-
-        if early_spans:
-            for c in range(len(early_spans)):
-                arrived(early_down(j), early_up(j), c)
-
-            def act_above(q, carry):
-                habove[j, q] = jnp.maximum(bn(zabove[j, q], norm), 0.0).astype(BF16)
-                return carry
-
-            def act_below(q, carry):
-                hbelow[j, q] = jnp.maximum(bn(zbelow[j, q], norm), 0.0).astype(BF16)
-                return carry
-
-            @pl.when(has_prev)
-            def _():
-                over((0, mid_early), act_above)
-
-            @pl.when(has_next)
-            def _():
-                over((0, mid_early), act_below)
-
         def layer_mid(q, acc):
             lhs = jnp.concatenate([u2[j, q], habove[j, q], hbelow[j, q]], axis=1)
             y = jnp.dot(lhs, wmid_ref[j], preferred_element_type=F32)
@@ -467,7 +390,7 @@
             zm[q] = z
             return add_stats(acc, z)
 
-        acc = over((0, mid_early), layer_mid, zero_acc)
+        acc = zero_acc
         for c, span in enumerate(mid_spans):
             arrived(mid_down(j), mid_up(j), c)
             acc = over(span, layer_mid, acc)
@@ -482,21 +405,15 @@
                 acc = add_stats(acc, z)
             return acc
 
-        acc = over(everything, layer_out, zero_acc, 2)
+        acc = over(everything, layer_out, zero_acc, 4)
         norm = norm_of(4 + 3 * j, group_stats(4 + 3 * j, acc, LANES), count_b)
-
-    def store(c):
-        part = pl.ds(*out_spans[c])
-        return pltpu.make_async_copy(h.at[:, part], out_hbm.at[:, part], out_sem.at[c])
 
     def final(q, carry):
         for a in range(2):
-            h[a, q] = jnp.maximum(bn(zo[a, q], norm) + h[a, q].astype(F32), 0.0).astype(BF16)
+            out_ref[a, q] = jnp.maximum(bn(zo[a, q], norm) + h[a, q].astype(F32), 0.0).astype(BF16)
         return carry
 
-    for c, span in enumerate(out_spans):
-        over(span, final)
-        store(c).start()
+    over(everything, final, 0, 2)
 
     for k in range(stats.shape[0]):
         to_dev(recv.at[k], recv.at[k], ssem.at[k], rsem.at[k], me).wait_send()
@@ -508,8 +425,6 @@
         for j in range(blocks):
             for c in range(len(mid_spans)):
                 mid_down(j)(c).wait_send()
-            for c in range(len(early_spans)):
-                early_down(j)(c).wait_send()
 
     @pl.when(has_prev)
     def _():
@@ -517,16 +432,9 @@
             img_up(c).wait_send()
         for c in range(len(row_spans)):
             row_up(c).wait_send()
-        if row_early:
-            early_row_up().wait_send()
         for j in range(blocks):
             for c in range(len(mid_spans)):
                 mid_up(j)(c).wait_send()
-            for c in range(len(early_spans)):
-                early_up(j)(c).wait_send()
-
-    for c in range(len(out_spans)):
-        store(c).wait()
 
 
 def solution(mesh):
@@ -536,7 +444,6 @@
         count, rows, width, chan_a = images.shape
         pairs, half_w = count // 2, width // 2
         blocks = w_in.shape[0]
-        row_early, mid_early = pairs * ROW_EARLY // OF_PAIRS, pairs * MID_EARLY // OF_PAIRS
         img = jnp.transpose(images, (0, 1, 3, 2)).reshape(2, pairs, rows, chan_a, width)
         taps = w_a.shape[1] * w_a.shape[2]
         raw = [
@@ -545,13 +452,12 @@
         ]
         steps = 2 + 3 * blocks
 
-        anyspace = pl.BlockSpec(memory_space=pl.ANY)
         dma = pltpu.SemaphoreType.DMA
         out = pl.pallas_call(
             functools.partial(kernel, n),
-            out_shape=jax.ShapeDtypeStruct((2, pairs, half_w, LANES), BF16),
+            out_shape=pltpu.VMEM((2, pairs, half_w, LANES), BF16),
             in_specs=[pl.BlockSpec(memory_space=pltpu.HBM)] * 11,
-            out_specs=anyspace,
+            out_specs=pl.BlockSpec(memory_space=pltpu.VMEM),
             scratch_shapes=[pltpu.VMEM(x.shape, x.dtype) for x in raw] + [
                 dma((len(raw),)),
                 pltpu.VMEM((2 * LANES, 4 * LANES), BF16),
@@ -569,16 +475,12 @@
                 pltpu.VMEM((2, pairs, half_w, LANES), F32),
                 pltpu.VMEM((pairs, half_w, LANES), BF16),
                 pltpu.VMEM((pairs, half_w, LANES), BF16),
-                pltpu.VMEM((row_early, half_w, LANES), F32),
-                pltpu.VMEM((row_early, half_w, LANES), F32),
                 pltpu.VMEM((2, pairs, half_w, LANES), F32),
                 pltpu.VMEM((2, pairs, half_w, LANES), BF16),
-                pltpu.VMEM((blocks, pairs, half_w, LANES), F32),
+                pltpu.VMEM((pairs, half_w, LANES), F32),
                 pltpu.VMEM((blocks, pairs, half_w, LANES), BF16),
                 pltpu.VMEM((blocks, pairs, half_w, LANES), BF16),
                 pltpu.VMEM((blocks, pairs, half_w, LANES), BF16),
-                pltpu.VMEM((blocks, mid_early, half_w, LANES), F32),
-                pltpu.VMEM((blocks, mid_early, half_w, LANES), F32),
                 pltpu.VMEM((pairs, half_w, LANES), F32),
                 pltpu.VMEM((2, pairs, half_w, LANES), F32),
                 pltpu.VMEM((steps, 2, LANES), F32),
@@ -588,18 +490,13 @@
                 dma((2, len(IMG_CUTS))),
                 dma((len(LATE_CUTS),)),
                 dma((len(LATE_CUTS),)),
-                dma,
-                dma,
                 dma((blocks, 2, len(LATE_CUTS))),
                 dma((blocks, 2, len(LATE_CUTS))),
-                dma((blocks, 2, len(EARLY_CUTS))),
-                dma((blocks, 2, len(EARLY_CUTS))),
                 dma((steps,)),
                 dma((steps,)),
-                dma((len(OUT_CUTS),)),
             ],
             compiler_params=pltpu.CompilerParams(
-                collective_id=0, has_side_effects=True, vmem_limit_bytes=60 * 1024 * 1024
+                collective_id=0, has_side_effects=True, vmem_limit_bytes=52 * 1024 * 1024
             ),
         )(img, *raw)
         return out.reshape(count, rows // 2, half_w, LANES)

time: 153 us -> 147 us (0.961)
  Pallas kernels: 150 us -> 145 us
  local copies, waits for them, and re-layouts: 3.14 us -> 1.32 us
    pallas_call x1, Pallas kernels: 150 us -> 145 us  [forward(): pl.pallas_call(functools.partial(kernel, n), out_shape=pltpu.VMEM((2, pai...]
    unnamed x1, local copies, waits for them, and re-layouts: 3.14 us -> 1.32 us
where the time goes in v5:
time: 147 us
  Pallas kernels  145 us (99%)
    pallas_call x1, Pallas kernels, forward(): pl.pallas_call(functools.partial(kernel, n), out_shape=pltpu.VMEM((2, pai...  145 us

profile of v5, /device:TPU:97, one launch (start us, length us, event | category | flops | bytes accessed | tf_op | source)
XLA Modules:
  0.0 146.7 jit_solution(5288765516651606572)
XLA Ops:
  0.0 145.3 %shard_map.109 = bf16[2,16,256,128]{3,2,1,0:T(8,128)(2,1)S(1)} custom-call(bf16[2,16,2,32,512]{4,3,2,1,0:T(8,128)(2,1)} %bitcast.11, bf16[288,32]{1,0:T(8,128)(2,1)} %bitcast.13, bf16[9,32,128]{2,1,0:T(8,128)(2,1)} %bitcast.14, bf16[3,64,128]{2,1,0:T(8,128)(2,1)} %bitcast.15, bf16[3,9,64,64]{3,2,1,0:T(8,128)(2,1)} %bitcast.12, bf16[3,64,128]{2,1,0:T(8,128)(2,1)} %wo_hbm.1, ...), custom_call_target="tpu_custom_call" | custom-call | tf_op jit(solution)/shard_map/pallas_call | solution.py:456
  145.3 1.3 copy.14

commit v6 on v5

--- a/solution.py
+++ b/solution.py
@@ -1,4 +1,5 @@
 import functools
+import math
 
 import jax
 import jax.numpy as jnp
@@ -43,6 +44,16 @@
     for q in range(start + trips * step, start + length):
         carry = body(q, carry)
     return carry
+
+
+def far_first(n):
+    side = max(1, math.isqrt(n // 2))
+
+    def hops(d):
+        x, y = d // 2 % side, d // (2 * side)
+        return min(x, side - x) + min(y, abs(side - y))
+
+    return sorted(range(1, n), key=lambda d: (-hops(d), d))
 
 
 def placement(size, copies):
@@ -156,6 +167,44 @@
     for copy in params[1:]:
         copy.start()
 
+    pl.semaphore_wait(barrier, n - 1)
+
+    def to_dev(src, dst, send_sem, recv_sem, dev):
+        return pltpu.make_async_remote_copy(
+            src_ref=src, dst_ref=dst, send_sem=send_sem, recv_sem=recv_sem, device_id={"sp": dev}, device_id_type=MESH
+        )
+
+    def img_down(c):
+        part = pl.ds(*img_spans[c])
+        return to_dev(ximg.at[:, part, 1], xabove.at[:, part], isend_sem.at[0, c], irecv_sem.at[0, c], nxt)
+
+    def img_up(c):
+        part = pl.ds(*img_spans[c])
+        return to_dev(ximg.at[:, part, 0], xbelow.at[:, part], isend_sem.at[1, c], irecv_sem.at[1, c], prv)
+
+    def exchange(down, up, c):
+        @pl.when(has_next)
+        def _():
+            down(c).start()
+
+        @pl.when(has_prev)
+        def _():
+            up(c).start()
+
+    def arrived(down, up, c):
+        @pl.when(has_prev)
+        def _():
+            down(c).wait_recv()
+
+        @pl.when(has_next)
+        def _():
+            up(c).wait_recv()
+
+    for copy in local_img:
+        copy.wait()
+    for c in range(len(img_spans)):
+        exchange(img_down, img_up, c)
+
     @pl.when(me == n - 1)
     def _():
         xbelow[...] = jnp.zeros_like(xbelow)
@@ -166,42 +215,6 @@
     def _():
         xabove[...] = jnp.zeros_like(xabove)
         habove[...] = jnp.zeros_like(habove)
-
-    pl.semaphore_wait(barrier, n - 1)
-
-    def to_dev(src, dst, send_sem, recv_sem, dev):
-        return pltpu.make_async_remote_copy(
-            src_ref=src, dst_ref=dst, send_sem=send_sem, recv_sem=recv_sem, device_id={"sp": dev}, device_id_type=MESH
-        )
-
-    def img_down(c):
-        part = pl.ds(*img_spans[c])
-        return to_dev(img_hbm.at[:, part, 1], xabove.at[:, part], isend_sem.at[0, c], irecv_sem.at[0, c], nxt)
-
-    def img_up(c):
-        part = pl.ds(*img_spans[c])
-        return to_dev(img_hbm.at[:, part, 0], xbelow.at[:, part], isend_sem.at[1, c], irecv_sem.at[1, c], prv)
-
-    def exchange(down, up, c):
-        @pl.when(has_next)
-        def _():
-            down(c).start()
-
-        @pl.when(has_prev)
-        def _():
-            up(c).start()
-
-    def arrived(down, up, c):
-        @pl.when(has_prev)
-        def _():
-            down(c).wait_recv()
-
-        @pl.when(has_next)
-        def _():
-            up(c).wait_recv()
-
-    for c in range(len(img_spans)):
-        exchange(img_down, img_up, c)
 
     params[0].wait()
     expand_stage_a(wa_raw[...], wao_ref, wah_ref)
@@ -230,7 +243,7 @@
 
         mine = jnp.concatenate([fold(acc[0]), fold(acc[1])], axis=0)
         stats[k] = mine
-        for d in sorted(range(1, n), key=lambda d: abs(2 * d - n)):
+        for d in far_first(n):
             to_dev(stats.at[k], recv.at[k, d - 1], ssem.at[k], rsem.at[k], lax.rem(me + d, n)).start()
         to_dev(recv.at[k], recv.at[k], ssem.at[k], rsem.at[k], me).wait_recv()
         return mine + jnp.sum(recv[k], axis=0)
@@ -265,9 +278,7 @@
         za[1, q] = z[:, LANES:]
         return carry
 
-    for c, span in enumerate(img_load):
-        local_img[c].wait()
-        over(span, own_a)
+    over(everything, own_a)
 
     for copy in params[1:]:
         copy.wait()

time: 147 us -> 147 us (level)
  no operation moved by 1% of the time
where the time goes in v6:
time: 147 us
  Pallas kernels  145 us (99%)
    pallas_call x1, Pallas kernels, forward(): pl.pallas_call(functools.partial(kernel, n), out_shape=pltpu.VMEM((2, pai...  145 us

profile of v6, /device:TPU:97, one launch (start us, length us, event | category | flops | bytes accessed | tf_op | source)
XLA Modules:
  0.0 146.6 jit_solution(18105937384803081270)
XLA Ops:
  0.0 145.3 %shard_map.109 = bf16[2,16,256,128]{3,2,1,0:T(8,128)(2,1)S(1)} custom-call(bf16[2,16,2,32,512]{4,3,2,1,0:T(8,128)(2,1)} %bitcast.11, bf16[288,32]{1,0:T(8,128)(2,1)} %bitcast.13, bf16[9,32,128]{2,1,0:T(8,128)(2,1)} %bitcast.14, bf16[3,64,128]{2,1,0:T(8,128)(2,1)} %bitcast.15, bf16[3,9,64,64]{3,2,1,0:T(8,128)(2,1)} %bitcast.12, bf16[3,64,128]{2,1,0:T(8,128)(2,1)} %wo_hbm.1, ...), custom_call_target="tpu_custom_call" | custom-call | tf_op jit(solution)/shard_map/pallas_call | solution.py:467
  145.3 1.3 copy.14

commit v7 on v6

--- a/solution.py
+++ b/solution.py
@@ -12,6 +12,7 @@
 MESH = pl.DeviceIdType.MESH
 LANES = 128
 IMG_CUTS = (5, 5, 4, 2)
+ROW_CUTS = (5, 5, 4, 2)
 LATE_CUTS = (5, 7, 3, 1)
 F32 = jnp.float32
 BF16 = jnp.bfloat16
@@ -65,7 +66,7 @@
     return hit.astype(F32).astype(BF16)
 
 
-def expand_stage_a(w, own_ref, halo_ref):
+def expand_stage_a(w, own_ref, halo_ref, third_ref):
     spread = jnp.dot(w, placement(32, 4), preferred_element_type=F32)
     own_ref[...] = jnp.zeros_like(own_ref)
     halo_ref[...] = jnp.zeros_like(halo_ref)
@@ -88,6 +89,20 @@
                     for a in range(2):
                         row, col = ((pi * 2 + a) * 2 + ri) * 32, (shift * 2 + a) * LANES
                         ref[row:row + 32, col:col + LANES] = block
+    third_ref[...] = jnp.zeros_like(third_ref)
+    for a in range(2):
+        for pi in range(2):
+            for ky in range(3):
+                for shift in range(2):
+                    total = jnp.zeros((32, LANES), F32)
+                    for po in range(2):
+                        if shift and pi == po:
+                            continue
+                        kx = (0 if pi == 1 else 2) if shift else pi - po + 1
+                        tap, i = ky * 3 + kx, a * 2 + po
+                        total += spread[tap * 32:(tap + 1) * 32, i * LANES:(i + 1) * LANES]
+                    row = ((a * 2 + pi) * 4 + ky) * 32
+                    third_ref[row:row + 32, shift * LANES:(shift + 1) * LANES] = total.astype(BF16)
 
 
 def expand_down(w_ref, own_ref, halo_ref):
@@ -126,25 +141,25 @@
 def kernel(
     n, img_hbm, wa_hbm, wd_hbm, wi_hbm, wm_hbm, wo_hbm, ba_hbm, bd_hbm, bi_hbm, bm_hbm, bo_hbm, out_ref,
     wa_raw, wd_raw, wi_raw, wm_raw, wo_raw, ba_raw, bd_raw, bi_raw, bm_raw, bo_raw, w_sem,
-    wao_ref, wah_ref, wdo_ref, wdh_ref, win_ref, wmid_ref, wout_ref, bn_ref,
-    ximg, xabove, xbelow, tscr, za, rsend, rrecv, zd, h, zi, u2, habove, hbelow,
+    wao_ref, wah_ref, wat_ref, wdo_ref, wdh_ref, win_ref, wmid_ref, wout_ref, bn_ref,
+    ximg, xabove, xbelow, tscr, za, zthird, rrow, zd, h, zi, u2, habove, hbelow,
     zm, zo, stats, recv,
-    img_sem, isend_sem, irecv_sem, rsend_sem, rrecv_sem, hsend_sem, hrecv_sem,
+    img_sem, isend_sem, irecv_sem, rowsend_sem, rowrecv_sem, hsend_sem, hrecv_sem,
     ssem, rsem,
 ):
     me = lax.axis_index("sp")
     nxt, prv = me + 1, me - 1
     has_next, has_prev = me < n - 1, me > 0
     pairs = ximg.shape[1]
-    half_w = tscr.shape[0] // 2
-    full_w = tscr.shape[0]
+    half_w = tscr.shape[1] // 2
+    full_w = tscr.shape[1]
     count_a = float(2 * pairs * 2 * full_w * n)
     count_b = float(2 * pairs * half_w * n)
     everything = (0, pairs)
 
     img_load = cuts(0, pairs, (4, 4, 4, 4))
     img_spans = cuts(0, pairs, IMG_CUTS)
-    row_spans = cuts(0, pairs, LATE_CUTS)
+    row_spans = cuts(0, pairs, ROW_CUTS)
     mid_spans = cuts(0, pairs, LATE_CUTS)
 
     params = [
@@ -180,7 +195,11 @@
 
     def img_up(c):
         part = pl.ds(*img_spans[c])
-        return to_dev(ximg.at[:, part, 0], xbelow.at[:, part], isend_sem.at[1, c], irecv_sem.at[1, c], prv)
+        return to_dev(ximg.at[:, part, 0], xbelow.at[:, part, 0], isend_sem.at[1, c], irecv_sem.at[1, c], prv)
+
+    def row_up(c):
+        part = pl.ds(*row_spans[c])
+        return to_dev(ximg.at[:, part, 1], xbelow.at[:, part, 1], rowsend_sem.at[c], rowrecv_sem.at[c], prv)
 
     def exchange(down, up, c):
         @pl.when(has_next)
@@ -204,11 +223,10 @@
         copy.wait()
     for c in range(len(img_spans)):
         exchange(img_down, img_up, c)
-
     @pl.when(me == n - 1)
     def _():
         xbelow[...] = jnp.zeros_like(xbelow)
-        rrecv[...] = jnp.zeros_like(rrecv)
+        rrow[...] = jnp.zeros_like(rrow)
         hbelow[...] = jnp.zeros_like(hbelow)
 
     @pl.when(me == 0)
@@ -217,7 +235,7 @@
         habove[...] = jnp.zeros_like(habove)
 
     params[0].wait()
-    expand_stage_a(wa_raw[...], wao_ref, wah_ref)
+    expand_stage_a(wa_raw[...], wao_ref, wah_ref, wat_ref)
 
     def shift_down(y):
         row = lax.broadcasted_iota(jnp.int32, y.shape, 0)
@@ -233,7 +251,7 @@
 
     zero_acc = (jnp.zeros((8, LANES), F32), jnp.zeros((8, LANES), F32))
 
-    def group_stats(k, acc, group):
+    def start_stats(k, acc, group):
         def fold(v):
             width = group
             while width < LANES:
@@ -245,8 +263,14 @@
         stats[k] = mine
         for d in far_first(n):
             to_dev(stats.at[k], recv.at[k, d - 1], ssem.at[k], rsem.at[k], lax.rem(me + d, n)).start()
+        return mine
+
+    def end_stats(k, mine):
         to_dev(recv.at[k], recv.at[k], ssem.at[k], rsem.at[k], me).wait_recv()
         return mine + jnp.sum(recv[k], axis=0)
+
+    def group_stats(k, acc, group):
+        return end_stats(k, start_stats(k, acc, group))
 
     def norm_of(k, total, count):
         moments = total * (1.0 / count)
@@ -262,14 +286,25 @@
     lane2 = lax.broadcasted_iota(jnp.int32, (half_w, 2 * LANES), 1)
     even_lane = lax.rem(lane2 // 32, 2) == 0
 
+    def split_parity(x, a):
+        tscr[a] = x.astype(F32).T
+        return [tscr[a, pl.ds(0, half_w, stride=2), :], tscr[a, pl.ds(1, half_w, stride=2), :]]
+
     def stage_a_part(x, w_ref):
-        tscr[...] = x.astype(F32).T
-        lhs = jnp.concatenate(
-            [tscr[pl.ds(0, half_w, stride=2), :], tscr[pl.ds(1, half_w, stride=2), :]], axis=1
-        ).astype(BF16)
+        lhs = jnp.concatenate(split_parity(x, 0), axis=1).astype(BF16)
         y = jnp.dot(lhs, w_ref[...], preferred_element_type=F32)
         cross = y[:, 2 * LANES:]
         return y[:, : 2 * LANES] + jnp.where(even_lane, shift_down(cross), shift_up(cross))
+
+    def third_row(q, carry):
+        parts = []
+        for a in range(2):
+            x = jnp.concatenate([ximg[a, q, 1], xbelow[a, q, 0], xbelow[a, q, 1], ximg[a, q, 0]], axis=0)
+            parts += split_parity(x, a)
+        y = jnp.dot(jnp.concatenate(parts, axis=1).astype(BF16), wat_ref[...], preferred_element_type=F32)
+        cross = y[:, LANES:]
+        zthird[q] = y[:, :LANES] + jnp.where(even_lane[:, :LANES], shift_down(cross), shift_up(cross))
+        return carry
 
     def own_a(q, carry):
         x = jnp.concatenate([ximg[0, q].reshape(2 * 32, full_w), ximg[1, q].reshape(2 * 32, full_w)], axis=0)
@@ -292,7 +327,7 @@
         bn_ref[4 + 3 * j] = bo_raw[j]
 
     def halo_a(q, acc):
-        x = jnp.concatenate([xabove[0, q], xbelow[0, q], xabove[1, q], xbelow[1, q]], axis=0)
+        x = jnp.concatenate([xabove[0, q], xbelow[0, q, 0], xabove[1, q], xbelow[1, q, 0]], axis=0)
         z = stage_a_part(x, wah_ref)
         z0 = za[0, q] + z[:, :LANES]
         z1 = za[1, q] + z[:, LANES:]
@@ -305,28 +340,18 @@
         arrived(img_down, img_up, c)
         acc = over(span, halo_a, acc)
 
-    lane1 = lax.broadcasted_iota(jnp.int32, (half_w, LANES), 1)
-    low_lane = lane1 < 64
-
-    def row_up(c):
-        part = pl.ds(*row_spans[c])
-        return to_dev(rsend.at[part], rrecv.at[part], rsend_sem.at[c], rrecv_sem.at[c], prv)
-
-    def first_rows(t0, t1):
-        return jnp.where(low_lane, t0, pltpu.roll(t1, 64, 1))
-
-    norm = norm_of(0, group_stats(0, acc, 32), count_a)
-
-    def pack_row(q, carry):
-        rsend[q] = jnp.maximum(bn(first_rows(za[0, q], za[1, q]), norm), 0.0).astype(BF16)
-        return carry
-
-    for c, span in enumerate(row_spans):
-        over(span, pack_row)
-
+    mine = start_stats(0, acc, 32)
+    for c in range(len(row_spans)):
         @pl.when(has_prev)
         def _():
             row_up(c).start()
+
+    @pl.when(has_next)
+    def _():
+        row_up(0).wait_recv()
+        over(row_spans[0], third_row)
+
+    norm = norm_of(0, end_stats(0, mine), count_a)
 
     def own_down(q, carry):
         for a in range(2):
@@ -338,7 +363,7 @@
     over(everything, own_down)
 
     def halo_down(q, acc):
-        y = jnp.dot(rrecv[q], wdh_ref[...], preferred_element_type=F32)
+        y = jnp.dot(rrow[q], wdh_ref[...], preferred_element_type=F32)
         for a in range(2):
             lo = 2 * a * LANES
             z = zd[a, q] + y[:, lo:lo + LANES] + shift_up(y[:, lo + LANES:lo + 2 * LANES])
@@ -346,11 +371,18 @@
             acc = add_stats(acc, z)
         return acc
 
+    def norm_row(q, carry):
+        rrow[q] = jnp.maximum(bn(zthird[q], norm), 0.0).astype(BF16)
+        return carry
+
     acc = zero_acc
     for c, span in enumerate(row_spans):
         @pl.when(has_next)
         def _():
-            row_up(c).wait_recv()
+            if c:
+                row_up(c).wait_recv()
+                over(span, third_row)
+            over(span, norm_row)
 
         acc = over(span, halo_down, acc)
     norm = norm_of(1, group_stats(1, acc, LANES), count_b)
@@ -473,6 +505,7 @@
                 dma((len(raw),)),
                 pltpu.VMEM((2 * LANES, 4 * LANES), BF16),
                 pltpu.VMEM((2 * LANES, 4 * LANES), BF16),
+                pltpu.VMEM((4 * LANES, 2 * LANES), BF16),
                 pltpu.VMEM((LANES, 2 * LANES), BF16),
                 pltpu.VMEM((LANES, 4 * LANES), BF16),
                 pltpu.VMEM((blocks, 2 * LANES, LANES), BF16),
@@ -481,10 +514,10 @@
                 pltpu.VMEM((steps, 2, LANES), F32),
                 pltpu.VMEM((2, pairs, rows, chan_a, width), BF16),
                 pltpu.VMEM((2, pairs, chan_a, width), BF16),
-                pltpu.VMEM((2, pairs, chan_a, width), BF16),
-                pltpu.VMEM((width, LANES), F32),
+                pltpu.VMEM((2, pairs, rows, chan_a, width), BF16),
+                pltpu.VMEM((2, width, LANES), F32),
                 pltpu.VMEM((2, pairs, half_w, LANES), F32),
-                pltpu.VMEM((pairs, half_w, LANES), BF16),
+                pltpu.VMEM((pairs, half_w, LANES), F32),
                 pltpu.VMEM((pairs, half_w, LANES), BF16),
                 pltpu.VMEM((2, pairs, half_w, LANES), F32),
                 pltpu.VMEM((2, pairs, half_w, LANES), BF16),
@@ -499,8 +532,8 @@
                 dma((4,)),
                 dma((2, len(IMG_CUTS))),
                 dma((2, len(IMG_CUTS))),
-                dma((len(LATE_CUTS),)),
-                dma((len(LATE_CUTS),)),
+                dma((len(ROW_CUTS),)),
+                dma((len(ROW_CUTS),)),
                 dma((blocks, 2, len(LATE_CUTS))),
                 dma((blocks, 2, len(LATE_CUTS))),
                 dma((steps,)),

time: 147 us -> 146 us (level)
  no operation moved by 1% of the time
where the time goes in v7:
time: 146 us
  Pallas kernels  145 us (99%)
    pallas_call x1, Pallas kernels, forward(): pl.pallas_call(functools.partial(kernel, n), out_shape=pltpu.VMEM((2, pai...  145 us

profile of v7, /device:TPU:97, one launch (start us, length us, event | category | flops | bytes accessed | tf_op | source)
XLA Modules:
  0.0 146.0 jit_solution(7387994040840898556)
XLA Ops:
  0.0 144.7 %shard_map.109 = bf16[2,16,256,128]{3,2,1,0:T(8,128)(2,1)S(1)} custom-call(bf16[2,16,2,32,512]{4,3,2,1,0:T(8,128)(2,1)} %bitcast.11, bf16[288,32]{1,0:T(8,128)(2,1)} %bitcast.13, bf16[9,32,128]{2,1,0:T(8,128)(2,1)} %bitcast.14, bf16[3,64,128]{2,1,0:T(8,128)(2,1)} %bitcast.15, bf16[3,9,64,64]{3,2,1,0:T(8,128)(2,1)} %bitcast.12, bf16[3,64,128]{2,1,0:T(8,128)(2,1)} %wo_hbm.1, ...), custom_call_target="tpu_custom_call" | custom-call | tf_op jit(solution)/shard_map/pallas_call | solution.py:499
  144.7 1.3 copy.14

commit v8 on v7

--- a/solution.py
+++ b/solution.py
@@ -13,6 +13,7 @@
 LANES = 128
 IMG_CUTS = (5, 5, 4, 2)
 ROW_CUTS = (5, 5, 4, 2)
+ROWS_AHEAD = 2
 LATE_CUTS = (5, 7, 3, 1)
 F32 = jnp.float32
 BF16 = jnp.bfloat16
@@ -105,18 +106,17 @@
                     third_ref[row:row + 32, shift * LANES:(shift + 1) * LANES] = total.astype(BF16)
 
 
-def expand_down(w_ref, own_ref, halo_ref):
-    own_ref[...] = jnp.zeros_like(own_ref)
-    halo_ref[...] = jnp.zeros_like(halo_ref)
+def expand_down(w_ref, down_ref):
+    down_ref[...] = jnp.zeros_like(down_ref)
     for par in range(2):
         for shift in range(2 - par):
-            kx = 2 if shift else par
-            for row in range(2):
-                at = (row * 2 + par) * 32
-                own_ref[at:at + 32, shift * LANES:(shift + 1) * LANES] = w_ref[row * 3 + kx]
+            kx, col = 2 if shift else par, shift * LANES
             for a in range(2):
-                at, col = (a * 2 + par) * 32, (a * 2 + shift) * LANES
-                halo_ref[at:at + 32, col:col + LANES] = w_ref[6 + kx]
+                for row in range(2):
+                    at = (row * 2 + par) * 32
+                    down_ref[a, at:at + 32, col:col + LANES] = w_ref[row * 3 + kx]
+                at = LANES + (a * 2 + par) * 32
+                down_ref[a, at:at + 32, col:col + LANES] = w_ref[6 + kx]
 
 
 def expand_blocks(w_in_ref, w_mid_ref, w_out_ref, win_ref, wmid_ref, wout_ref):
@@ -141,8 +141,8 @@
 def kernel(
     n, img_hbm, wa_hbm, wd_hbm, wi_hbm, wm_hbm, wo_hbm, ba_hbm, bd_hbm, bi_hbm, bm_hbm, bo_hbm, out_ref,
     wa_raw, wd_raw, wi_raw, wm_raw, wo_raw, ba_raw, bd_raw, bi_raw, bm_raw, bo_raw, w_sem,
-    wao_ref, wah_ref, wat_ref, wdo_ref, wdh_ref, win_ref, wmid_ref, wout_ref, bn_ref,
-    ximg, xabove, xbelow, tscr, za, zthird, rrow, zd, h, zi, u2, habove, hbelow,
+    wao_ref, wah_ref, wat_ref, wdn_ref, win_ref, wmid_ref, wout_ref, bn_ref,
+    ximg, xabove, xbelow, tscr, za, zthird, zd, h, zi, u2, habove, hbelow,
     zm, zo, stats, recv,
     img_sem, isend_sem, irecv_sem, rowsend_sem, rowrecv_sem, hsend_sem, hrecv_sem,
     ssem, rsem,
@@ -226,7 +226,7 @@
     @pl.when(me == n - 1)
     def _():
         xbelow[...] = jnp.zeros_like(xbelow)
-        rrow[...] = jnp.zeros_like(rrow)
+        zthird[...] = jnp.zeros_like(zthird)
         hbelow[...] = jnp.zeros_like(hbelow)
 
     @pl.when(me == 0)
@@ -317,7 +317,7 @@
 
     for copy in params[1:]:
         copy.wait()
-    expand_down(wd_raw, wdo_ref, wdh_ref)
+    expand_down(wd_raw, wdn_ref)
     expand_blocks(wi_raw, wm_raw, wo_raw, win_ref, wmid_ref, wout_ref)
     bn_ref[0] = jnp.concatenate([ba_raw[0]] * 4, axis=1)
     bn_ref[1] = bd_raw[...]
@@ -348,43 +348,31 @@
 
     @pl.when(has_next)
     def _():
-        row_up(0).wait_recv()
-        over(row_spans[0], third_row)
+        for c, span in enumerate(row_spans[:ROWS_AHEAD]):
+            row_up(c).wait_recv()
+            over(span, third_row)
 
     norm = norm_of(0, end_stats(0, mine), count_a)
 
-    def own_down(q, carry):
+    def down(q, acc):
+        third = jnp.where(has_next, jnp.maximum(bn(zthird[q], norm), 0.0), 0.0).astype(BF16)
         for a in range(2):
-            t = jnp.maximum(bn(za[a, q], norm), 0.0).astype(BF16)
-            y = jnp.dot(t, wdo_ref[...], preferred_element_type=F32)
-            zd[a, q] = y[:, :LANES] + shift_up(y[:, LANES:])
-        return carry
-
-    over(everything, own_down)
-
-    def halo_down(q, acc):
-        y = jnp.dot(rrow[q], wdh_ref[...], preferred_element_type=F32)
-        for a in range(2):
-            lo = 2 * a * LANES
-            z = zd[a, q] + y[:, lo:lo + LANES] + shift_up(y[:, lo + LANES:lo + 2 * LANES])
+            own = jnp.maximum(bn(za[a, q], norm), 0.0).astype(BF16)
+            y = jnp.dot(jnp.concatenate([own, third], axis=1), wdn_ref[a], preferred_element_type=F32)
+            z = y[:, :LANES] + shift_up(y[:, LANES:])
             zd[a, q] = z
             acc = add_stats(acc, z)
         return acc
 
-    def norm_row(q, carry):
-        rrow[q] = jnp.maximum(bn(zthird[q], norm), 0.0).astype(BF16)
-        return carry
-
     acc = zero_acc
     for c, span in enumerate(row_spans):
-        @pl.when(has_next)
-        def _():
-            if c:
+        if c >= ROWS_AHEAD:
+            @pl.when(has_next)
+            def _():
                 row_up(c).wait_recv()
                 over(span, third_row)
-            over(span, norm_row)
-
-        acc = over(span, halo_down, acc)
+
+        acc = over(span, down, acc)
     norm = norm_of(1, group_stats(1, acc, LANES), count_b)
 
     blocks = win_ref.shape[0]
@@ -506,8 +494,7 @@
                 pltpu.VMEM((2 * LANES, 4 * LANES), BF16),
                 pltpu.VMEM((2 * LANES, 4 * LANES), BF16),
                 pltpu.VMEM((4 * LANES, 2 * LANES), BF16),
-                pltpu.VMEM((LANES, 2 * LANES), BF16),
-                pltpu.VMEM((LANES, 4 * LANES), BF16),
+                pltpu.VMEM((2, 2 * LANES, 2 * LANES), BF16),
                 pltpu.VMEM((blocks, 2 * LANES, LANES), BF16),
                 pltpu.VMEM((blocks, 3 * LANES, 3 * LANES), BF16),
                 pltpu.VMEM((blocks, LANES, 2 * LANES), BF16),
@@ -518,7 +505,6 @@
                 pltpu.VMEM((2, width, LANES), F32),
                 pltpu.VMEM((2, pairs, half_w, LANES), F32),
                 pltpu.VMEM((pairs, half_w, LANES), F32),
-                pltpu.VMEM((pairs, half_w, LANES), BF16),
                 pltpu.VMEM((2, pairs, half_w, LANES), F32),
                 pltpu.VMEM((2, pairs, half_w, LANES), BF16),
                 pltpu.VMEM((pairs, half_w, LANES), F32),

time: 146 us -> 145 us (level)
  Pallas kernels: 145 us -> 143 us
    pallas_call x1, Pallas kernels: 145 us -> 143 us  [forward(): pl.pallas_call(functools.partial(kernel, n), out_shape=pltpu.VMEM((2, pai...]
where the time goes in v8:
time: 145 us; the launch traced here: 144 us
  Pallas kernels  143 us (99%)
    pallas_call x1, Pallas kernels, forward(): pl.pallas_call(functools.partial(kernel, n), out_shape=pltpu.VMEM((2, pai...  143 us

profile of v8, /device:TPU:97, one launch (start us, length us, event | category | flops | bytes accessed | tf_op | source)
XLA Modules:
  0.0 144.4 jit_solution(11570044117164147505)
XLA Ops:
  0.0 143.1 %shard_map.109 = bf16[2,16,256,128]{3,2,1,0:T(8,128)(2,1)S(1)} custom-call(bf16[2,16,2,32,512]{4,3,2,1,0:T(8,128)(2,1)} %bitcast.11, bf16[288,32]{1,0:T(8,128)(2,1)} %bitcast.13, bf16[9,32,128]{2,1,0:T(8,128)(2,1)} %bitcast.14, bf16[3,64,128]{2,1,0:T(8,128)(2,1)} %bitcast.15, bf16[3,9,64,64]{3,2,1,0:T(8,128)(2,1)} %bitcast.12, bf16[3,64,128]{2,1,0:T(8,128)(2,1)} %wo_hbm.1, ...), custom_call_target="tpu_custom_call" | custom-call | tf_op jit(solution)/shard_map/pallas_call | solution.py:487
  143.1 1.3 copy.14

commit v9 on v8

--- a/solution.py
+++ b/solution.py
@@ -11,10 +11,10 @@
 NORM_EPS = 1e-5
 MESH = pl.DeviceIdType.MESH
 LANES = 128
-IMG_CUTS = (5, 5, 4, 2)
-ROW_CUTS = (5, 5, 4, 2)
+IMG_CUTS = (6, 5, 4, 1)
+ROW_CUTS = (6, 5, 4, 1)
 ROWS_AHEAD = 2
-LATE_CUTS = (5, 7, 3, 1)
+LATE_CUTS = (3, 7, 5, 1)
 F32 = jnp.float32
 BF16 = jnp.bfloat16
 
@@ -174,11 +174,11 @@
         for c, span in enumerate(img_load)
     ]
     barrier = pltpu.get_barrier_semaphore()
-    for d in range(1, n):
+    for copy in local_img:
+        copy.start()
+    for d in far_first(n):
         pl.semaphore_signal(barrier, inc=1, device_id={"sp": lax.rem(me + d, n)}, device_id_type=MESH)
     params[0].start()
-    for copy in local_img:
-        copy.start()
     for copy in params[1:]:
         copy.start()
 

time: 145 us -> 147 us (1.014)
  Pallas kernels: 143 us -> 145 us
    pallas_call x1, Pallas kernels: 143 us -> 145 us  [forward(): pl.pallas_call(functools.partial(kernel, n), out_shape=pltpu.VMEM((2, pai...]
where the time goes in v9:
time: 147 us
  Pallas kernels  145 us (99%)
    pallas_call x1, Pallas kernels, forward(): pl.pallas_call(functools.partial(kernel, n), out_shape=pltpu.VMEM((2, pai...  145 us

profile of v9, /device:TPU:97, one launch (start us, length us, event | category | flops | bytes accessed | tf_op | source)
XLA Modules:
  0.0 146.5 jit_solution(16689000019334228759)
XLA Ops:
  0.0 145.2 %shard_map.109 = bf16[2,16,256,128]{3,2,1,0:T(8,128)(2,1)S(1)} custom-call(bf16[2,16,2,32,512]{4,3,2,1,0:T(8,128)(2,1)} %bitcast.11, bf16[288,32]{1,0:T(8,128)(2,1)} %bitcast.13, bf16[9,32,128]{2,1,0:T(8,128)(2,1)} %bitcast.14, bf16[3,64,128]{2,1,0:T(8,128)(2,1)} %bitcast.15, bf16[3,9,64,64]{3,2,1,0:T(8,128)(2,1)} %bitcast.12, bf16[3,64,128]{2,1,0:T(8,128)(2,1)} %wo_hbm.1, ...), custom_call_target="tpu_custom_call" | custom-call | tf_op jit(solution)/shard_map/pallas_call | solution.py:487
  145.2 1.3 copy.14

commit v10 on v8

--- a/solution.py
+++ b/solution.py
@@ -1,5 +1,4 @@
 import functools
-import math
 
 import jax
 import jax.numpy as jnp
@@ -14,7 +13,7 @@
 IMG_CUTS = (5, 5, 4, 2)
 ROW_CUTS = (5, 5, 4, 2)
 ROWS_AHEAD = 2
-LATE_CUTS = (5, 7, 3, 1)
+LATE_CUTS = (8, 6, 2)
 F32 = jnp.float32
 BF16 = jnp.bfloat16
 
@@ -49,13 +48,7 @@
 
 
 def far_first(n):
-    side = max(1, math.isqrt(n // 2))
-
-    def hops(d):
-        x, y = d // 2 % side, d // (2 * side)
-        return min(x, side - x) + min(y, abs(side - y))
-
-    return sorted(range(1, n), key=lambda d: (-hops(d), d))
+    return sorted(range(1, n), key=lambda d: abs(2 * d - n))
 
 
 def placement(size, copies):

time: 145 us -> 146 us (level)
  Pallas kernels: 143 us -> 145 us
    pallas_call x1, Pallas kernels: 143 us -> 145 us  [forward(): pl.pallas_call(functools.partial(kernel, n), out_shape=pltpu.VMEM((2, pai...]
where the time goes in v10:
time: 146 us
  Pallas kernels  145 us (99%)
    pallas_call x1, Pallas kernels, forward(): pl.pallas_call(functools.partial(kernel, n), out_shape=pltpu.VMEM((2, pai...  145 us

profile of v10, /device:TPU:97, one launch (start us, length us, event | category | flops | bytes accessed | tf_op | source)
XLA Modules:
  0.0 146.3 jit_solution(12696829819591445249)
XLA Ops:
  0.0 145.0 %shard_map.109 = bf16[2,16,256,128]{3,2,1,0:T(8,128)(2,1)S(1)} custom-call(bf16[2,16,2,32,512]{4,3,2,1,0:T(8,128)(2,1)} %bitcast.11, bf16[288,32]{1,0:T(8,128)(2,1)} %bitcast.13, bf16[9,32,128]{2,1,0:T(8,128)(2,1)} %bitcast.14, bf16[3,64,128]{2,1,0:T(8,128)(2,1)} %bitcast.15, bf16[3,9,64,64]{3,2,1,0:T(8,128)(2,1)} %bitcast.12, bf16[3,64,128]{2,1,0:T(8,128)(2,1)} %wo_hbm.1, ...), custom_call_target="tpu_custom_call" | custom-call | tf_op jit(solution)/shard_map/pallas_call | solution.py:480
  145.0 1.3 copy.14
